TPU v7x, 256 devices: a whole 4x4x8 slice. The times are simulated.
256 devices in a mesh: expert: 64 (over x, z, core), mp: 4 (over y).
Axes of the slice: x: 4, y: 4, z: 8, core: 2. Of those that a mesh axis runs over, the one named last changes fastest.
Arguments:
- tokens: bfloat16 [1536, 6144], P('expert', 'mp'), may hold values from -6 to 6
- mix_weights: float32 [1536, 2], P('expert'), may hold values from 0.2 to 1
- routes: int32 [1536, 2], P('expert'), may hold values from 0 to 7, as said below
- w_gate: bfloat16 [64, 6144, 1024], P('expert', None, 'mp'), may hold values from -0.078125 to 0.078125
- w_up: bfloat16 [64, 6144, 1024], P('expert', None, 'mp'), may hold values from -0.078125 to 0.078125
- w_down: bfloat16 [64, 1024, 6144], P('expert', 'mp'), may hold values from -0.0625 to 0.0625
Outputs:
- mixed_out: bfloat16 [1536, 6144], P('expert', 'mp')
Inputs may be any that keep to these rules, and one draw needn't show every extreme that they name: `routes`: each row names 2 different experts, and every expert is named by some row. Among the 24 rows of one index of the expert axis no expert is named more than 12 times, and on some indices one is named exactly 12 times.
All inputs are finite; a program needn't handle non-finite values.
Results may differ from a plain program's by a relative error of at most 0.011.
Values may be sent and summed in bfloat16 or wider, within the bound.
No kernel may reach another device: no remote copies, remote signals or barrier semaphores. Data moves between devices by JAX's collectives and lax.ppermute only.
A program may use at most 128 MiB of HBM per device.

v0:
```python
import math

import jax
import jax.numpy as jnp
from jax import lax
from jax.experimental import pallas as pl
from jax.experimental.pallas import tpu as pltpu
from jax.sharding import Mesh
from jax.sharding import PartitionSpec as P


EXPERTS = 8
TOP = 2
EXPERT = ("x", "z", "c")
SWAP = [(0, 1), (1, 0)]
BF = jnp.bfloat16
F32 = jnp.float32


def swap_cores(value):
    return lax.ppermute(value, "c", SWAP)


def shift(value, axis, by):
    size = lax.axis_size(axis)
    return lax.ppermute(value, axis, [(i, (i + by) % size) for i in range(size)])


def shift_y(value, by):
    return shift(value, "y", by)


def to_lanes(value):
    n, r, f = value.shape
    return jnp.swapaxes(value.reshape(n, r, f // 128, 128), 1, 2).reshape(n, f // 128 * r, 128)


VMEM = pl.BlockSpec(memory_space=pltpu.VMEM)


def near(value):
    return pltpu.with_memory_space_constraint(value, pltpu.VMEM)


def column(at):
    off, peer = at
    size = lax.axis_size("y")
    core = lax.axis_index("c")
    return (lax.axis_index("y") + off + size) % size * 2 + (1 - core if peer else core)


def cost(flops, *shapes):
    moved = sum(math.prod(shape) * 2 for shape in shapes)
    return pl.CostEstimate(flops=flops, transcendentals=0, bytes_accessed=moved)


def gate_up_body(pieces, ats, first, sends, *refs):
    xs = refs[: len(pieces)]
    gate_w, up_w = refs[len(pieces) : len(pieces) + 2]
    refs = refs[len(pieces) + 2 :]
    if not first:
        gate_in, up_in = refs[:2]
        refs = refs[2:]
    if sends:
        down_w = refs[0]
        outs = refs[1 : 1 + len(sends)]
        gate_acc, up_acc = refs[1 + len(sends) :]
    else:
        gate_acc, up_acc = refs
    block = xs[0].shape[1]
    done = set()
    for x_ref, (j, low, high) in zip(xs, pieces):
        rows = pl.ds(pl.multiple_of(column(ats[j]) * block, block), block)
        x = x_ref[...]
        g = jnp.dot(x, gate_w[rows, :], preferred_element_type=F32)
        u = jnp.dot(x, up_w[rows, :], preferred_element_type=F32)
        if low in done:
            gate_acc[low:high, :] += g
            up_acc[low:high, :] += u
        elif first:
            gate_acc[low:high, :] = g
            up_acc[low:high, :] = u
        else:
            gate_acc[low:high, :] = gate_in[low:high, :] + g
            up_acc[low:high, :] = up_in[low:high, :] + u
        done.add(low)
    if not sends:
        return
    gate = gate_acc[...]
    hidden = (gate / (1.0 + jnp.exp(-gate)) * up_acc[...]).astype(BF)
    for j, at in enumerate(sends):
        cols = pl.ds(pl.multiple_of(column(at) * block, 128), block)
        outs[j][...] = jnp.dot(hidden, down_w[:, cols], preferred_element_type=F32).astype(BF)


def gate_up(xs, pieces, ats, gate_rows, up_rows, carried, rows, down_rows=None, sends=()):
    block = xs[0].shape[1]
    units = gate_rows.shape[1]
    first = carried is None
    if sends:
        out = [pltpu.VMEM((rows, block), BF)] * len(sends)
    else:
        out = [pltpu.VMEM((rows, units), F32)] * 2
    n = len(ats)

    def body(*refs):
        gate_up_body(pieces, ats, first, sends, *refs)

    inputs = [*xs, gate_rows, up_rows]
    inputs += [] if first else carried
    inputs += [down_rows] if sends else []
    return pl.pallas_call(
        body,
        out_shape=out,
        in_specs=[VMEM] * len(inputs),
        out_specs=[VMEM] * len(out),
        scratch_shapes=[pltpu.VMEM((rows, units), F32)] * 2 if sends else [],
        compiler_params=pltpu.CompilerParams(vmem_limit_bytes=16 * 2**20),
        cost_estimate=cost(
            2 * rows * block * units * (2 * n + len(sends)),
            (2 * n + len(sends), block, units), (n + len(sends), rows, block), (8, rows, units),
        ),
        name="gate_up_down" if sends else "gate_up",
    )(*[near(v) for v in inputs])


def layer(tokens, mix_weights, routes, w_gate, w_up, w_down):
    tok_rows, width = tokens.shape
    xs, zs = lax.axis_size("x"), lax.axis_size("z")
    chips = xs * zs
    holders = chips // EXPERTS
    half = width // 2
    most = tok_rows // 2
    rows = 2 * most
    capacity = 5 * tok_rows * chips * 2 * TOP // (4 * EXPERTS)
    core = lax.axis_index("c")

    labels = jnp.arange(EXPERTS, dtype=jnp.int32)
    flat_ids = routes.reshape(-1)
    marked = (flat_ids[:, None] == labels[None, :]).astype(jnp.int32)
    earlier = jnp.cumsum(marked, axis=0) - marked
    rank = jnp.sum(earlier * marked, axis=1)
    counts = jnp.sum(marked, axis=0)
    place = flat_ids * rows + core * most + rank
    hit = (place[:, None] == jnp.arange(EXPERTS * rows, dtype=jnp.int32)[None, :]).reshape(
        tok_rows, TOP, EXPERTS * rows
    )
    pick = jnp.any(hit, axis=1).astype(BF)
    combine = jnp.sum(jnp.where(hit, mix_weights[:, :, None], jnp.zeros((), F32)), axis=1)

    packed = jnp.einsum("tp,tf->pf", pick, tokens, preferred_element_type=F32).astype(BF)
    packed = packed.reshape(EXPERTS, rows, width)
    meta = jnp.where(
        jnp.arange(8, dtype=jnp.int32)[None, :, None] == core, counts[:, None, None], 0
    ).astype(BF)
    meta = jnp.broadcast_to(meta, (EXPERTS, 8, 128))
    mine = lax.dynamic_slice_in_dim(packed, core * half, half, axis=2)
    peers = lax.dynamic_slice_in_dim(packed, (1 - core) * half, half, axis=2)
    mine = jnp.concatenate([meta, to_lanes(mine)], axis=1)
    peers = jnp.concatenate([meta, to_lanes(peers)], axis=1)
    blocks = mine + swap_cores(peers)
    combine_peer = swap_cores(combine)
    spread = jnp.broadcast_to(blocks[:, None], (EXPERTS, holders, *blocks.shape[1:]))
    arrived = lax.all_to_all(
        spread.reshape(chips, *blocks.shape[1:]), ("x", "z"), 0, 0, tiled=True
    )

    arrived_counts = arrived[:, 0:2, 0].astype(jnp.int32).reshape(-1)
    starts = jnp.cumsum(arrived_counts) - arrived_counts
    within = jnp.arange(most, dtype=jnp.int32)
    slot_of = jnp.where(
        within[None, :] < arrived_counts[:, None], starts[:, None] + within[None, :], -1
    ).reshape(-1)
    one_hot = (jnp.arange(capacity, dtype=jnp.int32)[:, None] == slot_of[None, :]).astype(BF)
    data = jnp.swapaxes(arrived[:, 8:].reshape(chips, half // 128, rows, 128), 1, 2)
    data = data.reshape(chips * rows, half)

    mid = capacity // 2
    gate_rows, up_rows, down_rows = w_gate[0], w_up[0], w_down[0]
    top = jnp.dot(one_hot[:mid], data, preferred_element_type=F32).astype(BF)
    bottom = jnp.dot(one_hot[mid:], data, preferred_element_type=F32).astype(BF)
    below_top = shift_y(top, 1)
    above_bottom = shift_y(bottom, -1)
    below_bottom = shift_y(bottom, 1)
    above_top = shift_y(top, -1)
    far_top = shift_y(below_top, 1)
    far_bottom = shift_y(above_bottom, -1)
    acts = gate_up(
        [top, bottom, swap_cores(top), swap_cores(bottom)],
        [(0, 0, mid), (0, mid, capacity), (1, 0, mid), (1, mid, capacity)],
        ((0, 0), (0, 1)),
        gate_rows, up_rows, None, capacity,
    )
    around = ((-1, 0), (1, 0), (-1, 1), (1, 1))
    for close, top_at, bottom_at in (
        ([below_top, above_bottom], 0, 1), ([above_top, below_bottom], 1, 0)
    ):
        acts = gate_up(
            close + [swap_cores(v) for v in close],
            [
                (top_at, 0, mid),
                (bottom_at, mid, capacity),
                (top_at + 2, 0, mid),
                (bottom_at + 2, mid, capacity),
            ],
            around,
            gate_rows, up_rows, acts, capacity,
        )
    far = [far_top, far_bottom]
    order = (2, 1, -1, 0)
    parts = gate_up(
        far + [swap_cores(v) for v in far],
        [(0, 0, mid), (0, mid, capacity), (1, 0, mid), (1, mid, capacity)],
        ((2, 0), (2, 1)),
        gate_rows, up_rows, acts, capacity,
        down_rows, tuple((off, 1) for off in order) + tuple((off, 0) for off in order),
    )

    def add(*values):
        return sum(v.astype(F32) for v in values).astype(BF)

    def chip_sums(k, peer):
        return lax.optimization_barrier(
            (add(parts[4 + k][:mid], peer[:mid]), add(parts[4 + k][mid:], peer[mid:]))
        )

    peers = [swap_cores(v) for v in parts[:4]]
    far_top, far_bottom = chip_sums(0, peers[0])
    top_in = shift_y(far_top, 1)
    bottom_in = shift_y(far_bottom, -1)
    up_top, up_bottom = chip_sums(1, peers[1])
    dn_top, dn_bottom = chip_sums(2, peers[2])
    below_bottom = shift_y(up_bottom, 1)
    above_top = shift_y(dn_top, -1)
    below_top = shift_y(lax.optimization_barrier(add(up_top, top_in)), 1)
    above_bottom = shift_y(lax.optimization_barrier(add(dn_bottom, bottom_in)), -1)
    part_own, peer_own = parts[7], peers[3]
    reduced = jnp.concatenate(
        [
            add(part_own[:mid], peer_own[:mid], below_top, above_top),
            add(part_own[mid:], peer_own[mid:], below_bottom, above_bottom),
        ]
    )

    back = lax.dot_general(
        one_hot, reduced, (((0,), (0,)), ((), ())), preferred_element_type=F32
    ).astype(BF)
    returned = lax.all_to_all(back.reshape(chips, rows, half), ("x", "z"), 0, 0, tiled=True)
    summed = jnp.sum(
        returned.reshape(EXPERTS, holders, rows, half).astype(F32), axis=1
    ).reshape(EXPERTS * rows, half)
    out_own = jnp.dot(combine, summed, precision=lax.Precision.HIGHEST).astype(BF)
    out_peer = jnp.dot(combine_peer, summed, precision=lax.Precision.HIGHEST).astype(BF)
    out_swap = swap_cores(out_peer)
    low = jnp.where(core == 0, out_own, out_swap)
    high = jnp.where(core == 0, out_swap, out_own)
    return jnp.concatenate([low, high], axis=1)


def solution(mesh):
    chips = Mesh(mesh.devices.reshape(4, 8, 2, mesh.shape["mp"]), ("x", "z", "c", "y"))
    placed = (
        P(EXPERT, "y"),
        P(EXPERT, None),
        P(EXPERT, None),
        P(EXPERT, None, "y"),
        P(EXPERT, None, "y"),
        P(EXPERT, "y", None),
    )
    return jax.shard_map(
        layer, mesh=chips, in_specs=placed, out_specs=P(EXPERT, "y"), check_vma=False
    )
```

profile of v0, /device:TPU:1, one launch (start us, length us, event | category | flops | bytes accessed | tf_op | source)
XLA Modules:
  0.0 162.8 jit_solution(4335592431474604107)
XLA Ops:
  3.2 3.3 %collective-permute-start = (bf16[8,152,128]{2,1,0:T(8,128)(2,1)S(1)}, bf16[8,152,128]{2,1,0:T(8,128)(2,1)S(1)}, u32[]{:S(2)}, u32[]{:S(2)}) collective-permute-start(bf16[8,152,128]{2,1,0:T(8,128)(2,1)S(1)} %pad_maximum_fusion), channel_id=1, source_target_pairs={{0,4},{4,0},{1,5},{5,1},{2,6},{6,2},{3,7},{7,3},{8,12},{12,8},{9,1... | collective-permute-start | bytes 933896 | tf_op jit(solution)/shard_map/ppermute | solution.py:21
  8.0 41.4 %all_to_all.10 = bf16[32,152,128]{2,1,0:T(8,128)(2,1)S(1)} all-to-all(bf16[32,152,128]{2,1,0:T(8,128)(2,1)S(1)} %bitcast.42), channel_id=1, replica_groups=mesh['x'=4,'z'=8,'c'=2,'y'=4] {'x','z'}, dimensions={0} | all-to-all | bytes 2490368 | tf_op jit(solution)/shard_map/all_to_all | solution.py:164
  51.8 2.3 %collective-permute-start.14 = (bf16[240,768]{1,0:T(8,128)(2,1)S(1)}, bf16[240,768]{1,0:T(8,128)(2,1)S(1)}, u32[]{:S(2)}, u32[]{:S(2)}) collective-permute-start(bf16[240,768]{1,0:T(8,128)(2,1)S(1)} %convolution_convert_fusion.2.refs_1_), channel_id=1, source_target_pairs={{0,4},{4,0},{1,5},{5,1},{2,6},{6,2},{3,7},{7,3},{8,12},{12,8},{9,1... | collective-permute-start | bytes 1105928 | tf_op jit(solution)/shard_map/ppermute | solution.py:21
  54.1 2.7 %collective-permute-start.3 = (bf16[240,768]{1,0:T(8,128)(2,1)S(1)}, bf16[240,768]{1,0:T(8,128)(2,1)S(1)}, u32[]{:S(2)}, u32[]{:S(2)}) collective-permute-start(bf16[240,768]{1,0:T(8,128)(2,1)S(1)} %convolution_convert_fusion.2.refs_1_), channel_id=1, source_target_pairs={{0,3},{1,0},{2,1},{3,2},{4,7},{5,4},{6,5},{7,6},{8,11},{9,8},{10,9... | collective-permute-start | bytes 1105928 | tf_op jit(solution)/shard_map/ppermute | solution.py:26
  57.7 2.7 %collective-permute-start.7 = (bf16[240,768]{1,0:T(8,128)(2,1)S(1)}, bf16[240,768]{1,0:T(8,128)(2,1)S(1)}, u32[]{:S(2)}, u32[]{:S(2)}) collective-permute-start(bf16[240,768]{1,0:T(8,128)(2,1)S(1)} %convolution_convert_fusion.3.refs_0_), channel_id=1, source_target_pairs={{0,3},{1,0},{2,1},{3,2},{4,7},{5,4},{6,5},{7,6},{8,11},{9,8},{10,9... | collective-permute-start | bytes 1105928 | tf_op jit(solution)/shard_map/ppermute | solution.py:26
  60.4 4.2 %collective-permute-done.3.refs_1_ = bf16[240,768]{1,0:T(8,128)(2,1)S(1)} collective-permute-done((bf16[240,768]{1,0:T(8,128)(2,1)S(1)}, bf16[240,768]{1,0:T(8,128)(2,1)S(1)}, u32[]{:S(2)}, u32[]{:S(2)}) %collective-permute-start.3) | collective-permute-done | bytes 368672 | tf_op jit(solution)/shard_map/ppermute | solution.py:26
  64.6 1.5 collective-permute-start.12
  66.1 3.4 %collective-permute-start.4 = (bf16[240,768]{1,0:T(8,128)(2,1)S(1)}, bf16[240,768]{1,0:T(8,128)(2,1)S(1)}, u32[]{:S(2)}, u32[]{:S(2)}) collective-permute-start(bf16[240,768]{1,0:T(8,128)(2,1)S(1)} %collective-permute-done.3.refs_1_), channel_id=1, source_target_pairs={{0,3},{1,0},{2,1},{3,2},{4,7},{5,4},{6,5},{7,6},{8,11},{9,8},{10,9... | collective-permute-start | bytes 1105928 | tf_op jit(solution)/shard_map/ppermute | solution.py:26
  69.6 7.3 %collective-permute-done.8.refs_1_ = bf16[240,768]{1,0:T(8,128)(2,1)S(1)} collective-permute-done((bf16[240,768]{1,0:T(8,128)(2,1)S(1)}, bf16[240,768]{1,0:T(8,128)(2,1)S(1)}, u32[]{:S(2)}, u32[]{:S(2)}) %collective-permute-start.8) | collective-permute-done | bytes 368672 | tf_op jit(solution)/shard_map/ppermute | solution.py:26
  76.8 1.6 collective-permute-start.11
  78.9 1.5 collective-permute-done.4.refs_1_
  81.4 3.3 %collective-permute-done.2.refs_0_ = bf16[240,768]{1,0:T(8,128)(2,1)S(1)} collective-permute-done((bf16[240,768]{1,0:T(8,128)(2,1)S(1)}, bf16[240,768]{1,0:T(8,128)(2,1)S(1)}, u32[]{:S(2)}, u32[]{:S(2)}) %collective-permute-start.2) | collective-permute-done | bytes 368672 | tf_op jit(solution)/shard_map/ppermute | solution.py:26
  89.5 2.5 %gate_up_down.1 = (bf16[480,768]{1,0:T(8,128)(2,1)S(1)}, bf16[480,768]{1,0:T(8,128)(2,1)S(1)}, bf16[480,768]{1,0:T(8,128)(2,1)S(1)}, bf16[480,768]{1,0:T(8,128)(...) custom-call(bf16[240,768]{1,0:T(8,128)(2,1)S(1)} %collective-permute, ...), custom_call_target="tpu_custom_call" | custom-call | flops 2264924160 | bytes 14057472 | tf_op jit(solution)/shard_map/gate_up_down/pallas_call | solution.py:112
  94.6 1.5 collective-permute-start.18
  96.7 2.7 %collective-permute-start.21 = (bf16[240,768]{1,0:T(8,128)(2,1)S(1)}, bf16[240,768]{1,0:T(8,128)(2,1)S(1)}, u32[]{:S(2)}, u32[]{:S(2)}) collective-permute-start(bf16[240,768]{1,0:T(8,128)(2,1)S(1)} %get-tuple-element.41), channel_id=1, source_target_pairs={{0,3},{1,0},{2,1},{3,2},{4,7},{5,4},{6,5},{7,6},{8,11},{9,8},{10,9... | collective-permute-start | bytes 1105928 | tf_op jit(solution)/shard_map/ppermute | solution.py:26
  99.4 5.2 %collective-permute-done.23 = bf16[240,768]{1,0:T(8,128)(2,1)S(1)} collective-permute-done((bf16[240,768]{1,0:T(8,128)(2,1)S(1)}, bf16[240,768]{1,0:T(8,128)(2,1)S(1)}, u32[]{:S(2)}, u32[]{:S(2)}) %collective-permute-start.23) | collective-permute-done | bytes 368672 | tf_op jit(solution)/shard_map/ppermute | solution.py:26
  104.7 1.8 %collective-permute-start.24 = (bf16[240,768]{1,0:T(8,128)(2,1)S(1)}, bf16[240,768]{1,0:T(8,128)(2,1)S(1)}, u32[]{:S(2)}, u32[]{:S(2)}) collective-permute-start(bf16[240,768]{1,0:T(8,128)(2,1)S(1)} %add_convert_fusion.1), channel_id=1, source_target_pairs={{0,3},{1,0},{2,1},{3,2},{4,7},{5,4},{6,5},{7,6},{8,11},{9,8},{10,9... | collective-permute-start | bytes 1105928 | tf_op jit(solution)/shard_map/ppermute | solution.py:26
  106.7 7.1 %collective-permute-done.22 = bf16[240,768]{1,0:T(8,128)(2,1)S(1)} collective-permute-done((bf16[240,768]{1,0:T(8,128)(2,1)S(1)}, bf16[240,768]{1,0:T(8,128)(2,1)S(1)}, u32[]{:S(2)}, u32[]{:S(2)}) %collective-permute-start.22) | collective-permute-done | bytes 368672 | tf_op jit(solution)/shard_map/ppermute | solution.py:26
  113.8 6.6 %collective-permute-done.24 = bf16[240,768]{1,0:T(8,128)(2,1)S(1)} collective-permute-done((bf16[240,768]{1,0:T(8,128)(2,1)S(1)}, bf16[240,768]{1,0:T(8,128)(2,1)S(1)}, u32[]{:S(2)}, u32[]{:S(2)}) %collective-permute-start.24) | collective-permute-done | bytes 368672 | tf_op jit(solution)/shard_map/ppermute | solution.py:26
  122.1 1.9 %convolution_convert_fusion.1 = bf16[768,768]{1,0:T(8,128)(2,1)} fusion(bf16[240,768]{1,0:T(8,128)(2,1)S(1)} %get-tuple-element.48, bf16[240,768]{1,0:T(8,128)(2,1)S(1)} %get-tuple-element.47, s32[768]{0:T(1024)S(1)} %select_n.48), kind=kOutput, calls=%fused_computation.2 | convolution fusion | flops 568664064 | bytes 1920000 | tf_op jit(solution)/shard_map/dot_general | solution.py:245
  124.0 4.2 %all-to-all-start.1 = ((bf16[32,24,768]{2,1,0:T(8,128)(2,1)}), bf16[32,24,768]{2,1,0:T(8,128)(2,1)S(1)}, u32[]{:S(2)}, u32[]{:S(2)}) async-start(bf16[32,24,768]{2,1,0:T(8,128)(2,1)} %bitcast.12), calls=%async_computation.1 | async-start | bytes 2359296 | tf_op jit(solution)/shard_map/all_to_all | solution.py:248
  128.3 1.4 collective-permute-start.25
  129.7 26.4 %all-to-all-done.1 = bf16[32,24,768]{2,1,0:T(8,128)(2,1)S(1)} async-done(((bf16[32,24,768]{2,1,0:T(8,128)(2,1)}), bf16[32,24,768]{2,1,0:T(8,128)(2,1)S(1)}, u32[]{:S(2)}, u32[]{:S(2)}) %all-to-all-start.1) | async-done | bytes 1179680 | tf_op jit(solution)/shard_map/all_to_all | solution.py:248
  156.7 4.6 %collective-permute-start.26 = (bf16[24,768]{1,0:T(8,128)(2,1)S(1)}, bf16[24,768]{1,0:T(8,128)(2,1)S(1)}, u32[]{:S(2)}, u32[]{:S(2)}) collective-permute-start(bf16[24,768]{1,0:T(8,128)(2,1)S(1)} %convolution_convert_fusion.4), channel_id=1, source_target_pairs={{0,4},{4,0},{1,5},{5,1},{2,6},{6,2},{3,7},{7,3},{8,12},{12,8},{9,1... | collective-permute-start | bytes 110600 | tf_op jit(solution)/shard_map/ppermute | solution.py:21
  (94 shorter events, 21.3 us)
Async XLA Ops:
  3.2 4.5 %collective-permute-start = (bf16[8,152,128]{2,1,0:T(8,128)(2,1)S(1)}, bf16[8,152,128]{2,1,0:T(8,128)(2,1)S(1)}, u32[]{:S(2)}, u32[]{:S(2)}) collective-permute-start(bf16[8,152,128]{2,1,0:T(8,128)(2,1)S(1)} %pad_maximum_fusion), channel_id=1, source_target_pairs={{0,4},{4,0},{1,5},{5,1},{2,6},{6,2},{3,7},{7,3},{8,12},{12,8},{9,1... | collective-permute-start | bytes 933896 | tf_op jit(solution)/shard_map/ppermute | solution.py:21
  51.8 6.0 %collective-permute-start.14 = (bf16[240,768]{1,0:T(8,128)(2,1)S(1)}, bf16[240,768]{1,0:T(8,128)(2,1)S(1)}, u32[]{:S(2)}, u32[]{:S(2)}) collective-permute-start(bf16[240,768]{1,0:T(8,128)(2,1)S(1)} %convolution_convert_fusion.2.refs_1_), channel_id=1, source_target_pairs={{0,4},{4,0},{1,5},{5,1},{2,6},{6,2},{3,7},{7,3},{8,12},{12,8},{9,1... | collective-permute-start | bytes 1105928 | tf_op jit(solution)/shard_map/ppermute | solution.py:21
  54.1 10.6 %collective-permute-start.3 = (bf16[240,768]{1,0:T(8,128)(2,1)S(1)}, bf16[240,768]{1,0:T(8,128)(2,1)S(1)}, u32[]{:S(2)}, u32[]{:S(2)}) collective-permute-start(bf16[240,768]{1,0:T(8,128)(2,1)S(1)} %convolution_convert_fusion.2.refs_1_), channel_id=1, source_target_pairs={{0,3},{1,0},{2,1},{3,2},{4,7},{5,4},{6,5},{7,6},{8,11},{9,8},{10,9... | collective-permute-start | bytes 1105928 | tf_op jit(solution)/shard_map/ppermute | solution.py:26
  57.3 8.9 %collective-permute-start.13 = (bf16[240,768]{1,0:T(8,128)(2,1)S(1)}, bf16[240,768]{1,0:T(8,128)(2,1)S(1)}, u32[]{:S(2)}, u32[]{:S(2)}) collective-permute-start(bf16[240,768]{1,0:T(8,128)(2,1)S(1)} %convolution_convert_fusion.3.refs_0_), channel_id=1, source_target_pairs={{0,4},{4,0},{1,5},{5,1},{2,6},{6,2},{3,7},{7,3},{8,12},{12,8},{9,1... | collective-permute-start | bytes 1105928 | tf_op jit(solution)/shard_map/ppermute | solution.py:21
  57.7 11.8 %collective-permute-start.1 = (bf16[240,768]{1,0:T(8,128)(2,1)S(1)}, bf16[240,768]{1,0:T(8,128)(2,1)S(1)}, u32[]{:S(2)}, u32[]{:S(2)}) collective-permute-start(bf16[240,768]{1,0:T(8,128)(2,1)S(1)} %convolution_convert_fusion.3.refs_0_), channel_id=1, source_target_pairs={{0,1},{1,2},{2,3},{3,0},{4,5},{5,6},{6,7},{7,4},{8,9},{9,10},{10,1... | collective-permute-start | bytes 1105928 | tf_op jit(solution)/shard_map/ppermute | solution.py:26
  57.7 19.1 %collective-permute-start.8 = (bf16[240,768]{1,0:T(8,128)(2,1)S(1)}, bf16[240,768]{1,0:T(8,128)(2,1)S(1)}, u32[]{:S(2)}, u32[]{:S(2)}) collective-permute-start(bf16[240,768]{1,0:T(8,128)(2,1)S(1)} %convolution_convert_fusion.2.refs_1_), channel_id=1, source_target_pairs={{0,1},{1,2},{2,3},{3,0},{4,5},{5,6},{6,7},{7,4},{8,9},{9,10},{10,1... | collective-permute-start | bytes 1105928 | tf_op jit(solution)/shard_map/ppermute | solution.py:26
  57.7 20.7 %collective-permute-start.7 = (bf16[240,768]{1,0:T(8,128)(2,1)S(1)}, bf16[240,768]{1,0:T(8,128)(2,1)S(1)}, u32[]{:S(2)}, u32[]{:S(2)}) collective-permute-start(bf16[240,768]{1,0:T(8,128)(2,1)S(1)} %convolution_convert_fusion.3.refs_0_), channel_id=1, source_target_pairs={{0,3},{1,0},{2,1},{3,2},{4,7},{5,4},{6,5},{7,6},{8,11},{9,8},{10,9... | collective-permute-start | bytes 1105928 | tf_op jit(solution)/shard_map/ppermute | solution.py:26
  64.6 13.8 %collective-permute-start.12 = (bf16[240,768]{1,0:T(8,128)(2,1)S(1)}, bf16[240,768]{1,0:T(8,128)(2,1)S(1)}, u32[]{:S(2)}, u32[]{:S(2)}) collective-permute-start(bf16[240,768]{1,0:T(8,128)(2,1)S(1)} %collective-permute-done.3.refs_1_), channel_id=1, source_target_pairs={{0,4},{4,0},{1,5},{5,1},{2,6},{6,2},{3,7},{7,3},{8,12},{12,8},{9,1... | collective-permute-start | bytes 1105928 | tf_op jit(solution)/shard_map/ppermute | solution.py:21
  66.1 14.3 %collective-permute-start.4 = (bf16[240,768]{1,0:T(8,128)(2,1)S(1)}, bf16[240,768]{1,0:T(8,128)(2,1)S(1)}, u32[]{:S(2)}, u32[]{:S(2)}) collective-permute-start(bf16[240,768]{1,0:T(8,128)(2,1)S(1)} %collective-permute-done.3.refs_1_), channel_id=1, source_target_pairs={{0,3},{1,0},{2,1},{3,2},{4,7},{5,4},{6,5},{7,6},{8,11},{9,8},{10,9... | collective-permute-start | bytes 1105928 | tf_op jit(solution)/shard_map/ppermute | solution.py:26
  69.6 15.2 %collective-permute-start.2 = (bf16[240,768]{1,0:T(8,128)(2,1)S(1)}, bf16[240,768]{1,0:T(8,128)(2,1)S(1)}, u32[]{:S(2)}, u32[]{:S(2)}) collective-permute-start(bf16[240,768]{1,0:T(8,128)(2,1)S(1)} %collective-permute-done.1.refs_0_), channel_id=1, source_target_pairs={{0,1},{1,2},{2,3},{3,0},{4,5},{5,6},{6,7},{7,4},{8,9},{9,10},{10,1... | collective-permute-start | bytes 1105928 | tf_op jit(solution)/shard_map/ppermute | solution.py:26
  76.8 9.8 %collective-permute-start.11 = (bf16[240,768]{1,0:T(8,128)(2,1)S(1)}, bf16[240,768]{1,0:T(8,128)(2,1)S(1)}, u32[]{:S(2)}, u32[]{:S(2)}) collective-permute-start(bf16[240,768]{1,0:T(8,128)(2,1)S(1)} %collective-permute-done.1.refs_0_), channel_id=1, source_target_pairs={{0,4},{4,0},{1,5},{5,1},{2,6},{6,2},{3,7},{7,3},{8,12},{12,8},{9,1... | collective-permute-start | bytes 1105928 | tf_op jit(solution)/shard_map/ppermute | solution.py:21
  78.4 9.2 %collective-permute-start.10 = (bf16[240,768]{1,0:T(8,128)(2,1)S(1)}, bf16[240,768]{1,0:T(8,128)(2,1)S(1)}, u32[]{:S(2)}, u32[]{:S(2)}) collective-permute-start(bf16[240,768]{1,0:T(8,128)(2,1)S(1)} %collective-permute-done.8.refs_1_), channel_id=1, source_target_pairs={{0,4},{4,0},{1,5},{5,1},{2,6},{6,2},{3,7},{7,3},{8,12},{12,8},{9,1... | collective-permute-start | bytes 1105928 | tf_op jit(solution)/shard_map/ppermute | solution.py:21
  78.4 9.2 %collective-permute-start.9 = (bf16[240,768]{1,0:T(8,128)(2,1)S(1)}, bf16[240,768]{1,0:T(8,128)(2,1)S(1)}, u32[]{:S(2)}, u32[]{:S(2)}) collective-permute-start(bf16[240,768]{1,0:T(8,128)(2,1)S(1)} %collective-permute-done.7.refs_0_), channel_id=1, source_target_pairs={{0,4},{4,0},{1,5},{5,1},{2,6},{6,2},{3,7},{7,3},{8,12},{12,8},{9,1... | collective-permute-start | bytes 1105928 | tf_op jit(solution)/shard_map/ppermute | solution.py:21
  80.4 8.2 %collective-permute-start.6 = (bf16[240,768]{1,0:T(8,128)(2,1)S(1)}, bf16[240,768]{1,0:T(8,128)(2,1)S(1)}, u32[]{:S(2)}, u32[]{:S(2)}) collective-permute-start(bf16[240,768]{1,0:T(8,128)(2,1)S(1)} %collective-permute-done.4.refs_1_), channel_id=1, source_target_pairs={{0,4},{4,0},{1,5},{5,1},{2,6},{6,2},{3,7},{7,3},{8,12},{12,8},{9,1... | collective-permute-start | bytes 1105928 | tf_op jit(solution)/shard_map/ppermute | solution.py:21
  92.8 13.9 %collective-permute-start.15 = (bf16[480,768]{1,0:T(8,128)(2,1)S(1)}, bf16[480,768]{1,0:T(8,128)(2,1)S(1)}, u32[]{:S(2)}, u32[]{:S(2)}) collective-permute-start(bf16[480,768]{1,0:T(8,128)(2,1)S(1)} %get-tuple-element.32), channel_id=1, source_target_pairs={{0,4},{4,0},{1,5},{5,1},{2,6},{6,2},{3,7},{7,3},{8,12},{12,8},{9,1... | collective-permute-start | bytes 2211848 | tf_op jit(solution)/shard_map/ppermute | solution.py:21
  94.5 10.1 %collective-permute-start.23 = (bf16[240,768]{1,0:T(8,128)(2,1)S(1)}, bf16[240,768]{1,0:T(8,128)(2,1)S(1)}, u32[]{:S(2)}, u32[]{:S(2)}) collective-permute-start(bf16[240,768]{1,0:T(8,128)(2,1)S(1)} %get-tuple-element.44), channel_id=1, source_target_pairs={{0,3},{1,0},{2,1},{3,2},{4,7},{5,4},{6,5},{7,6},{8,11},{9,8},{10,9... | collective-permute-start | bytes 1105928 | tf_op jit(solution)/shard_map/ppermute | solution.py:26
  94.6 11.9 %collective-permute-start.18 = (bf16[240,768]{1,0:T(8,128)(2,1)S(1)}, bf16[240,768]{1,0:T(8,128)(2,1)S(1)}, u32[]{:S(2)}, u32[]{:S(2)}) collective-permute-start(bf16[240,768]{1,0:T(8,128)(2,1)S(1)} %get-tuple-element.38), channel_id=1, source_target_pairs={{0,1},{1,2},{2,3},{3,0},{4,5},{5,6},{6,7},{7,4},{8,9},{9,10},{10,1... | collective-permute-start | bytes 1105928 | tf_op jit(solution)/shard_map/ppermute | solution.py:26
  96.7 17.2 %collective-permute-start.22 = (bf16[240,768]{1,0:T(8,128)(2,1)S(1)}, bf16[240,768]{1,0:T(8,128)(2,1)S(1)}, u32[]{:S(2)}, u32[]{:S(2)}) collective-permute-start(bf16[240,768]{1,0:T(8,128)(2,1)S(1)} %get-tuple-element.42), channel_id=1, source_target_pairs={{0,1},{1,2},{2,3},{3,0},{4,5},{5,6},{6,7},{7,4},{8,9},{9,10},{10,1... | collective-permute-start | bytes 1105928 | tf_op jit(solution)/shard_map/ppermute | solution.py:26
  96.7 17.1 %collective-permute-start.21 = (bf16[240,768]{1,0:T(8,128)(2,1)S(1)}, bf16[240,768]{1,0:T(8,128)(2,1)S(1)}, u32[]{:S(2)}, u32[]{:S(2)}) collective-permute-start(bf16[240,768]{1,0:T(8,128)(2,1)S(1)} %get-tuple-element.41), channel_id=1, source_target_pairs={{0,3},{1,0},{2,1},{3,2},{4,7},{5,4},{6,5},{7,6},{8,11},{9,8},{10,9... | collective-permute-start | bytes 1105928 | tf_op jit(solution)/shard_map/ppermute | solution.py:26
  104.7 15.7 %collective-permute-start.24 = (bf16[240,768]{1,0:T(8,128)(2,1)S(1)}, bf16[240,768]{1,0:T(8,128)(2,1)S(1)}, u32[]{:S(2)}, u32[]{:S(2)}) collective-permute-start(bf16[240,768]{1,0:T(8,128)(2,1)S(1)} %add_convert_fusion.1), channel_id=1, source_target_pairs={{0,3},{1,0},{2,1},{3,2},{4,7},{5,4},{6,5},{7,6},{8,11},{9,8},{10,9... | collective-permute-start | bytes 1105928 | tf_op jit(solution)/shard_map/ppermute | solution.py:26
  106.6 15.1 %collective-permute-start.19 = (bf16[240,768]{1,0:T(8,128)(2,1)S(1)}, bf16[240,768]{1,0:T(8,128)(2,1)S(1)}, u32[]{:S(2)}, u32[]{:S(2)}) collective-permute-start(bf16[240,768]{1,0:T(8,128)(2,1)S(1)} %add_convert_fusion.5), channel_id=1, source_target_pairs={{0,1},{1,2},{2,3},{3,0},{4,5},{5,6},{6,7},{7,4},{8,9},{9,10},{10,1... | collective-permute-start | bytes 1105928 | tf_op jit(solution)/shard_map/ppermute | solution.py:26
  124.0 32.1 %all-to-all-start.1 = ((bf16[32,24,768]{2,1,0:T(8,128)(2,1)}), bf16[32,24,768]{2,1,0:T(8,128)(2,1)S(1)}, u32[]{:S(2)}, u32[]{:S(2)}) async-start(bf16[32,24,768]{2,1,0:T(8,128)(2,1)} %bitcast.12), calls=%async_computation.1 | async-start | bytes 2359296 | tf_op jit(solution)/shard_map/all_to_all | solution.py:248
  128.3 27.9 %collective-permute-start.25 = (f32[24,192]{1,0:T(8,128)S(1)}, f32[24,192]{1,0:T(8,128)S(1)}, u32[]{:S(2)}, u32[]{:S(2)}) collective-permute-start(f32[24,192]{1,0:T(8,128)S(1)} %select_reduce_fusion), channel_id=1, source_target_pairs={{0,4},{4,0},{1,5},{5,1},{2,6},{6,2},{3,7},{7,3},{8,12},{12,8},{9,1... | collective-permute-start | bytes 55304 | tf_op jit(solution)/shard_map/ppermute | solution.py:21
  156.7 5.5 %collective-permute-start.26 = (bf16[24,768]{1,0:T(8,128)(2,1)S(1)}, bf16[24,768]{1,0:T(8,128)(2,1)S(1)}, u32[]{:S(2)}, u32[]{:S(2)}) collective-permute-start(bf16[24,768]{1,0:T(8,128)(2,1)S(1)} %convolution_convert_fusion.4), channel_id=1, source_target_pairs={{0,4},{4,0},{1,5},{5,1},{2,6},{6,2},{3,7},{7,3},{8,12},{12,8},{9,1... | collective-permute-start | bytes 110600 | tf_op jit(solution)/shard_map/ppermute | solution.py:21
  (9 other events, 91.6 us)
where the time goes:
time: 163 us
  waiting for transfers between devices  65.7 us (40%)
  blocking collectives  41.4 us (25%)
  starting transfers between devices  37.9 us (23%)
  Pallas kernels  5.32 us (3%)
  other arithmetic  4.41 us (3%)
  matrix products  3.95 us (2%)
  local copies, waits for them, and re-layouts  3.73 us (2%)
    all_to_all x1, blocking collectives, layer(): lax.all_to_all(spread.reshape(chips, *blocks.shape[1:]), ('x', 'z'), 0, 0...  41.4 us
    ppermute x12, waiting for transfers between devices, shift(): lax.ppermute(value, axis, [(i, (i + by) % size) for i in range(size)])  36.6 us
    all_to_all x1, waiting for transfers between devices, layer(): lax.all_to_all(back.reshape(chips, rows, half), ('x', 'z'), 0, 0, tiled=T...  26.4 us
    ppermute x15, starting transfers between devices, swap_cores(): return lax.ppermute(value, 'c', SWAP)  18.7 us
    ppermute x12, starting transfers between devices, shift(): lax.ppermute(value, axis, [(i, (i + by) % size) for i in range(size)])  15 us
    pallas_call x4, Pallas kernels, gate_up(): pl.pallas_call(body, out_shape=out, in_specs=[VMEM] * len(inputs), out_sp...  5.32 us
    all_to_all x1, starting transfers between devices, layer(): lax.all_to_all(back.reshape(chips, rows, half), ('x', 'z'), 0, 0, tiled=T...  4.25 us
  transfers between devices with their start and end apart: 28, of which 13 were waited for; matrix products, arithmetic and copies ran while one was open for 1% of the time, Pallas kernels for 2%

commit v1 on v0

--- a/solution.py
+++ b/solution.py
@@ -11,6 +11,7 @@
 
 EXPERTS = 8
 TOP = 2
+EMPTY = 256.0
 EXPERT = ("x", "z", "c")
 SWAP = [(0, 1), (1, 0)]
 BF = jnp.bfloat16
@@ -28,11 +29,6 @@
 
 def shift_y(value, by):
     return shift(value, "y", by)
-
-
-def to_lanes(value):
-    n, r, f = value.shape
-    return jnp.swapaxes(value.reshape(n, r, f // 128, 128), 1, 2).reshape(n, f // 128 * r, 128)
 
 
 VMEM = pl.BlockSpec(memory_space=pltpu.VMEM)
@@ -52,6 +48,67 @@
 def cost(flops, *shapes):
     moved = sum(math.prod(shape) * 2 for shape in shapes)
     return pl.CostEstimate(flops=flops, transcendentals=0, bytes_accessed=moved)
+
+
+def pack_body(routes_ref, tokens_ref, mine_ref, peers_ref, stage):
+    tok_rows, width = tokens_ref.shape
+    rows = tok_rows
+    most = tok_rows // 2
+    half = width // 2
+    slots = EXPERTS * rows
+    core = lax.axis_index("c")
+
+    def iota(shape, dim):
+        return lax.broadcasted_iota(jnp.int32, shape, dim)
+
+    experts = iota((tok_rows, EXPERTS), 1)
+    hits = (routes_ref[:, 0:1] == experts) | (routes_ref[:, 1:2] == experts)
+    hits = hits.astype(F32)
+    before = (iota((tok_rows, tok_rows), 1) < iota((tok_rows, tok_rows), 0)).astype(F32)
+    rank = jnp.dot(before, hits, preferred_element_type=F32)
+    counts = jnp.dot(jnp.ones((8, tok_rows), F32), hits, preferred_element_type=F32)
+    lane = iota((EXPERTS, slots), 1)
+    low = iota((EXPERTS, slots), 0) * rows
+    expand = ((lane >= low) & (lane < low + rows)).astype(F32)
+
+    def place(n):
+        at = iota((n, slots), 1)
+        first = sum((at >= e * rows).astype(jnp.int32) for e in range(1, EXPERTS)) * rows
+        return at - first - core * most
+
+    hit = jnp.dot(hits, expand, preferred_element_type=F32) > 0.5
+    rank = jnp.dot(rank, expand, preferred_element_type=F32).astype(jnp.int32)
+    counts = jnp.dot(counts, expand, preferred_element_type=F32).astype(jnp.int32)
+    pick = jnp.where(hit & (rank == place(tok_rows)), 1.0, 0.0).astype(BF)
+    empty = (place(8) >= counts) & (place(8) < most) & (iota((8, slots), 0) == 0)
+    empty = jnp.where(empty, 1.0, 0.0).astype(BF)
+    over_rows = (((0,), (0,)), ((), ()))
+    stage[...] = lax.dot_general(
+        pick, tokens_ref[...], over_rows, preferred_element_type=F32
+    ) + lax.dot_general(
+        empty, jnp.full((8, width), EMPTY, BF), over_rows, preferred_element_type=F32
+    )
+    for e in range(EXPERTS):
+        for f in range(half // 128):
+            for out, side in ((mine_ref, core), (peers_ref, 1 - core)):
+                lanes = pl.ds(pl.multiple_of(side * half + f * 128, 128), 128)
+                out[e, f * rows : (f + 1) * rows, :] = stage[
+                    e * rows : (e + 1) * rows, lanes
+                ].astype(BF)
+
+
+def pack(routes, tokens):
+    tok_rows, width = tokens.shape
+    out = pltpu.VMEM((EXPERTS, width // 256 * tok_rows, 128), BF)
+    return pl.pallas_call(
+        pack_body,
+        out_shape=[out, out],
+        in_specs=[VMEM] * 2,
+        out_specs=[VMEM] * 2,
+        scratch_shapes=[pltpu.VMEM((EXPERTS * tok_rows, width), F32)],
+        compiler_params=pltpu.CompilerParams(vmem_limit_bytes=16 * 2**20),
+        name="pack",
+    )(near(routes), near(tokens))
 
 
 def gate_up_body(pieces, ats, first, sends, *refs):
@@ -140,7 +197,6 @@
     marked = (flat_ids[:, None] == labels[None, :]).astype(jnp.int32)
     earlier = jnp.cumsum(marked, axis=0) - marked
     rank = jnp.sum(earlier * marked, axis=1)
-    counts = jnp.sum(marked, axis=0)
     place = flat_ids * rows + core * most + rank
     hit = (place[:, None] == jnp.arange(EXPERTS * rows, dtype=jnp.int32)[None, :]).reshape(
         tok_rows, TOP, EXPERTS * rows
@@ -148,16 +204,7 @@
     pick = jnp.any(hit, axis=1).astype(BF)
     combine = jnp.sum(jnp.where(hit, mix_weights[:, :, None], jnp.zeros((), F32)), axis=1)
 
-    packed = jnp.einsum("tp,tf->pf", pick, tokens, preferred_element_type=F32).astype(BF)
-    packed = packed.reshape(EXPERTS, rows, width)
-    meta = jnp.where(
-        jnp.arange(8, dtype=jnp.int32)[None, :, None] == core, counts[:, None, None], 0
-    ).astype(BF)
-    meta = jnp.broadcast_to(meta, (EXPERTS, 8, 128))
-    mine = lax.dynamic_slice_in_dim(packed, core * half, half, axis=2)
-    peers = lax.dynamic_slice_in_dim(packed, (1 - core) * half, half, axis=2)
-    mine = jnp.concatenate([meta, to_lanes(mine)], axis=1)
-    peers = jnp.concatenate([meta, to_lanes(peers)], axis=1)
+    mine, peers = pack(routes, tokens)
     blocks = mine + swap_cores(peers)
     combine_peer = swap_cores(combine)
     spread = jnp.broadcast_to(blocks[:, None], (EXPERTS, holders, *blocks.shape[1:]))
@@ -165,14 +212,15 @@
         spread.reshape(chips, *blocks.shape[1:]), ("x", "z"), 0, 0, tiled=True
     )
 
-    arrived_counts = arrived[:, 0:2, 0].astype(jnp.int32).reshape(-1)
+    filled = (arrived[:, :rows, 0].astype(F32) < EMPTY / 2).astype(jnp.int32)
+    arrived_counts = jnp.sum(filled.reshape(chips * 2, most), axis=1)
     starts = jnp.cumsum(arrived_counts) - arrived_counts
     within = jnp.arange(most, dtype=jnp.int32)
     slot_of = jnp.where(
         within[None, :] < arrived_counts[:, None], starts[:, None] + within[None, :], -1
     ).reshape(-1)
     one_hot = (jnp.arange(capacity, dtype=jnp.int32)[:, None] == slot_of[None, :]).astype(BF)
-    data = jnp.swapaxes(arrived[:, 8:].reshape(chips, half // 128, rows, 128), 1, 2)
+    data = jnp.swapaxes(arrived.reshape(chips, half // 128, rows, 128), 1, 2)
     data = data.reshape(chips * rows, half)
 
     mid = capacity // 2

time: 163 us -> 162 us (level)
  no operation moved by 1% of the time
where the time goes in v1:
time: 162 us; the launch traced here: 161 us
  waiting for transfers between devices  65.4 us (40%)
  blocking collectives  40.9 us (25%)
  starting transfers between devices  37.6 us (23%)
  Pallas kernels  6.22 us (4%)
  local copies, waits for them, and re-layouts  3.65 us (2%)
  other arithmetic  3.62 us (2%)
  matrix products  3.59 us (2%)
    all_to_all x1, blocking collectives, layer(): lax.all_to_all(spread.reshape(chips, *blocks.shape[1:]), ('x', 'z'), 0, 0...  40.9 us
    ppermute x12, waiting for transfers between devices, shift(): lax.ppermute(value, axis, [(i, (i + by) % size) for i in range(size)])  36.6 us
    all_to_all x1, waiting for transfers between devices, layer(): lax.all_to_all(back.reshape(chips, rows, half), ('x', 'z'), 0, 0, tiled=T...  25.7 us
    ppermute x15, starting transfers between devices, swap_cores(): return lax.ppermute(value, 'c', SWAP)  18.5 us
    ppermute x12, starting transfers between devices, shift(): lax.ppermute(value, axis, [(i, (i + by) % size) for i in range(size)])  15 us
    pallas_call x4, Pallas kernels, gate_up(): pl.pallas_call(body, out_shape=out, in_specs=[VMEM] * len(inputs), out_sp...  5.32 us
    all_to_all x1, starting transfers between devices, layer(): lax.all_to_all(back.reshape(chips, rows, half), ('x', 'z'), 0, 0, tiled=T...  4.07 us
  transfers between devices with their start and end apart: 28, of which 13 were waited for; matrix products, arithmetic and copies ran while one was open for 1% of the time, Pallas kernels for 2%

profile of v1, /device:TPU:1, one launch (start us, length us, event | category | flops | bytes accessed | tf_op | source)
XLA Modules:
  0.0 161.4 jit_solution(8112989097721856910)
XLA Ops:
  2.5 3.3 %collective-permute-start = (bf16[8,144,128]{2,1,0:T(8,128)(2,1)S(1)}, bf16[8,144,128]{2,1,0:T(8,128)(2,1)S(1)}, u32[]{:S(2)}, u32[]{:S(2)}) collective-permute-start(bf16[8,144,128]{2,1,0:T(8,128)(2,1)S(1)} %get-tuple-element.28), channel_id=1, source_target_pairs={{0,4},{4,0},{1,5},{5,1},{2,6},{6,2},{3,7},{7,3},{8,12},{12,8},{9,1... | collective-permute-start | bytes 884744 | tf_op jit(solution)/shard_map/ppermute | solution.py:22
  7.3 40.9 %all_to_all.10 = bf16[32,144,128]{2,1,0:T(8,128)(2,1)S(1)} all-to-all(bf16[32,144,128]{2,1,0:T(8,128)(2,1)S(1)} %bitcast.36), channel_id=1, replica_groups=mesh['x'=4,'z'=8,'c'=2,'y'=4] {'x','z'}, dimensions={0} | all-to-all | bytes 2359296 | tf_op jit(solution)/shard_map/all_to_all | solution.py:211
  50.7 2.2 %collective-permute-start.14 = (bf16[240,768]{1,0:T(8,128)(2,1)S(1)}, bf16[240,768]{1,0:T(8,128)(2,1)S(1)}, u32[]{:S(2)}, u32[]{:S(2)}) collective-permute-start(bf16[240,768]{1,0:T(8,128)(2,1)S(1)} %convolution_convert_fusion.1.refs_1_), channel_id=1, source_target_pairs={{0,4},{4,0},{1,5},{5,1},{2,6},{6,2},{3,7},{7,3},{8,12},{12,8},{9,1... | collective-permute-start | bytes 1105928 | tf_op jit(solution)/shard_map/ppermute | solution.py:22
  52.9 2.7 %collective-permute-start.3 = (bf16[240,768]{1,0:T(8,128)(2,1)S(1)}, bf16[240,768]{1,0:T(8,128)(2,1)S(1)}, u32[]{:S(2)}, u32[]{:S(2)}) collective-permute-start(bf16[240,768]{1,0:T(8,128)(2,1)S(1)} %convolution_convert_fusion.1.refs_1_), channel_id=1, source_target_pairs={{0,3},{1,0},{2,1},{3,2},{4,7},{5,4},{6,5},{7,6},{8,11},{9,8},{10,9... | collective-permute-start | bytes 1105928 | tf_op jit(solution)/shard_map/ppermute | solution.py:27
  56.6 2.7 %collective-permute-start.7 = (bf16[240,768]{1,0:T(8,128)(2,1)S(1)}, bf16[240,768]{1,0:T(8,128)(2,1)S(1)}, u32[]{:S(2)}, u32[]{:S(2)}) collective-permute-start(bf16[240,768]{1,0:T(8,128)(2,1)S(1)} %convolution_convert_fusion.2.refs_0_), channel_id=1, source_target_pairs={{0,3},{1,0},{2,1},{3,2},{4,7},{5,4},{6,5},{7,6},{8,11},{9,8},{10,9... | collective-permute-start | bytes 1105928 | tf_op jit(solution)/shard_map/ppermute | solution.py:27
  59.2 4.2 %collective-permute-done.3.refs_1_ = bf16[240,768]{1,0:T(8,128)(2,1)S(1)} collective-permute-done((bf16[240,768]{1,0:T(8,128)(2,1)S(1)}, bf16[240,768]{1,0:T(8,128)(2,1)S(1)}, u32[]{:S(2)}, u32[]{:S(2)}) %collective-permute-start.3) | collective-permute-done | bytes 368672 | tf_op jit(solution)/shard_map/ppermute | solution.py:27
  63.5 1.5 collective-permute-start.12
  65.0 3.4 %collective-permute-start.4 = (bf16[240,768]{1,0:T(8,128)(2,1)S(1)}, bf16[240,768]{1,0:T(8,128)(2,1)S(1)}, u32[]{:S(2)}, u32[]{:S(2)}) collective-permute-start(bf16[240,768]{1,0:T(8,128)(2,1)S(1)} %collective-permute-done.3.refs_1_), channel_id=1, source_target_pairs={{0,3},{1,0},{2,1},{3,2},{4,7},{5,4},{6,5},{7,6},{8,11},{9,8},{10,9... | collective-permute-start | bytes 1105928 | tf_op jit(solution)/shard_map/ppermute | solution.py:27
  68.4 7.3 %collective-permute-done.8.refs_1_ = bf16[240,768]{1,0:T(8,128)(2,1)S(1)} collective-permute-done((bf16[240,768]{1,0:T(8,128)(2,1)S(1)}, bf16[240,768]{1,0:T(8,128)(2,1)S(1)}, u32[]{:S(2)}, u32[]{:S(2)}) %collective-permute-start.8) | collective-permute-done | bytes 368672 | tf_op jit(solution)/shard_map/ppermute | solution.py:27
  75.6 1.6 collective-permute-start.11
  77.8 1.5 collective-permute-done.4.refs_1_
  80.2 3.3 %collective-permute-done.2.refs_0_ = bf16[240,768]{1,0:T(8,128)(2,1)S(1)} collective-permute-done((bf16[240,768]{1,0:T(8,128)(2,1)S(1)}, bf16[240,768]{1,0:T(8,128)(2,1)S(1)}, u32[]{:S(2)}, u32[]{:S(2)}) %collective-permute-start.2) | collective-permute-done | bytes 368672 | tf_op jit(solution)/shard_map/ppermute | solution.py:27
  88.3 2.5 %gate_up_down.1 = (bf16[480,768]{1,0:T(8,128)(2,1)S(1)}, bf16[480,768]{1,0:T(8,128)(2,1)S(1)}, bf16[480,768]{1,0:T(8,128)(2,1)S(1)}, bf16[480,768]{1,0:T(8,128)(...) custom-call(bf16[240,768]{1,0:T(8,128)(2,1)S(1)} %collective-permute, ...), custom_call_target="tpu_custom_call" | custom-call | flops 2264924160 | bytes 14057472 | tf_op jit(solution)/shard_map/gate_up_down/pallas_call | solution.py:169
  93.4 1.5 collective-permute-start.18
  95.5 2.7 %collective-permute-start.21 = (bf16[240,768]{1,0:T(8,128)(2,1)S(1)}, bf16[240,768]{1,0:T(8,128)(2,1)S(1)}, u32[]{:S(2)}, u32[]{:S(2)}) collective-permute-start(bf16[240,768]{1,0:T(8,128)(2,1)S(1)} %get-tuple-element.45), channel_id=1, source_target_pairs={{0,3},{1,0},{2,1},{3,2},{4,7},{5,4},{6,5},{7,6},{8,11},{9,8},{10,9... | collective-permute-start | bytes 1105928 | tf_op jit(solution)/shard_map/ppermute | solution.py:27
  98.2 5.2 %collective-permute-done.23 = bf16[240,768]{1,0:T(8,128)(2,1)S(1)} collective-permute-done((bf16[240,768]{1,0:T(8,128)(2,1)S(1)}, bf16[240,768]{1,0:T(8,128)(2,1)S(1)}, u32[]{:S(2)}, u32[]{:S(2)}) %collective-permute-start.23) | collective-permute-done | bytes 368672 | tf_op jit(solution)/shard_map/ppermute | solution.py:27
  103.5 1.6 collective-permute-start.24
  105.5 7.1 %collective-permute-done.22 = bf16[240,768]{1,0:T(8,128)(2,1)S(1)} collective-permute-done((bf16[240,768]{1,0:T(8,128)(2,1)S(1)}, bf16[240,768]{1,0:T(8,128)(2,1)S(1)}, u32[]{:S(2)}, u32[]{:S(2)}) %collective-permute-start.22) | collective-permute-done | bytes 368672 | tf_op jit(solution)/shard_map/ppermute | solution.py:27
  112.6 6.6 %collective-permute-done.24 = bf16[240,768]{1,0:T(8,128)(2,1)S(1)} collective-permute-done((bf16[240,768]{1,0:T(8,128)(2,1)S(1)}, bf16[240,768]{1,0:T(8,128)(2,1)S(1)}, u32[]{:S(2)}, u32[]{:S(2)}) %collective-permute-start.24) | collective-permute-done | bytes 368672 | tf_op jit(solution)/shard_map/ppermute | solution.py:27
  119.2 1.3 collective-permute-done.19
  120.9 1.9 %convolution_convert_fusion = bf16[768,768]{1,0:T(8,128)(2,1)} fusion(bf16[240,768]{1,0:T(8,128)(2,1)S(1)} %get-tuple-element.50, bf16[240,768]{1,0:T(8,128)(2,1)S(1)} %get-tuple-element.49, s32[768]{0:T(1024)S(1)} %select_n.30), kind=kOutput, calls=%fused_computation.1 | convolution fusion | flops 568664064 | bytes 1920000 | tf_op jit(solution)/shard_map/dot_general | solution.py:293
  122.8 4.1 %all-to-all-start.1 = ((bf16[32,24,768]{2,1,0:T(8,128)(2,1)}), bf16[32,24,768]{2,1,0:T(8,128)(2,1)S(1)}, u32[]{:S(2)}, u32[]{:S(2)}) async-start(bf16[32,24,768]{2,1,0:T(8,128)(2,1)} %bitcast.7), calls=%async_computation.1 | async-start | bytes 2359296 | tf_op jit(solution)/shard_map/all_to_all | solution.py:296
  128.7 25.7 %all-to-all-done.1 = bf16[32,24,768]{2,1,0:T(8,128)(2,1)S(1)} async-done(((bf16[32,24,768]{2,1,0:T(8,128)(2,1)}), bf16[32,24,768]{2,1,0:T(8,128)(2,1)S(1)}, u32[]{:S(2)}, u32[]{:S(2)}) %all-to-all-start.1) | async-done | bytes 1179680 | tf_op jit(solution)/shard_map/all_to_all | solution.py:296
  155.0 4.8 %collective-permute-start.26 = (bf16[24,768]{1,0:T(8,128)(2,1)S(1)}, bf16[24,768]{1,0:T(8,128)(2,1)S(1)}, u32[]{:S(2)}, u32[]{:S(2)}) collective-permute-start(bf16[24,768]{1,0:T(8,128)(2,1)S(1)} %convolution_convert_fusion.3), channel_id=1, source_target_pairs={{0,4},{4,0},{1,5},{5,1},{2,6},{6,2},{3,7},{7,3},{8,12},{12,8},{9,1... | collective-permute-start | bytes 110600 | tf_op jit(solution)/shard_map/ppermute | solution.py:22
  (86 shorter events, 21.4 us)
Async XLA Ops:
  2.5 4.5 %collective-permute-start = (bf16[8,144,128]{2,1,0:T(8,128)(2,1)S(1)}, bf16[8,144,128]{2,1,0:T(8,128)(2,1)S(1)}, u32[]{:S(2)}, u32[]{:S(2)}) collective-permute-start(bf16[8,144,128]{2,1,0:T(8,128)(2,1)S(1)} %get-tuple-element.28), channel_id=1, source_target_pairs={{0,4},{4,0},{1,5},{5,1},{2,6},{6,2},{3,7},{7,3},{8,12},{12,8},{9,1... | collective-permute-start | bytes 884744 | tf_op jit(solution)/shard_map/ppermute | solution.py:22
  50.7 5.9 %collective-permute-start.14 = (bf16[240,768]{1,0:T(8,128)(2,1)S(1)}, bf16[240,768]{1,0:T(8,128)(2,1)S(1)}, u32[]{:S(2)}, u32[]{:S(2)}) collective-permute-start(bf16[240,768]{1,0:T(8,128)(2,1)S(1)} %convolution_convert_fusion.1.refs_1_), channel_id=1, source_target_pairs={{0,4},{4,0},{1,5},{5,1},{2,6},{6,2},{3,7},{7,3},{8,12},{12,8},{9,1... | collective-permute-start | bytes 1105928 | tf_op jit(solution)/shard_map/ppermute | solution.py:22
  52.9 10.6 %collective-permute-start.3 = (bf16[240,768]{1,0:T(8,128)(2,1)S(1)}, bf16[240,768]{1,0:T(8,128)(2,1)S(1)}, u32[]{:S(2)}, u32[]{:S(2)}) collective-permute-start(bf16[240,768]{1,0:T(8,128)(2,1)S(1)} %convolution_convert_fusion.1.refs_1_), channel_id=1, source_target_pairs={{0,3},{1,0},{2,1},{3,2},{4,7},{5,4},{6,5},{7,6},{8,11},{9,8},{10,9... | collective-permute-start | bytes 1105928 | tf_op jit(solution)/shard_map/ppermute | solution.py:27
  56.1 8.9 %collective-permute-start.13 = (bf16[240,768]{1,0:T(8,128)(2,1)S(1)}, bf16[240,768]{1,0:T(8,128)(2,1)S(1)}, u32[]{:S(2)}, u32[]{:S(2)}) collective-permute-start(bf16[240,768]{1,0:T(8,128)(2,1)S(1)} %convolution_convert_fusion.2.refs_0_), channel_id=1, source_target_pairs={{0,4},{4,0},{1,5},{5,1},{2,6},{6,2},{3,7},{7,3},{8,12},{12,8},{9,1... | collective-permute-start | bytes 1105928 | tf_op jit(solution)/shard_map/ppermute | solution.py:22
  56.5 11.8 %collective-permute-start.1 = (bf16[240,768]{1,0:T(8,128)(2,1)S(1)}, bf16[240,768]{1,0:T(8,128)(2,1)S(1)}, u32[]{:S(2)}, u32[]{:S(2)}) collective-permute-start(bf16[240,768]{1,0:T(8,128)(2,1)S(1)} %convolution_convert_fusion.2.refs_0_), channel_id=1, source_target_pairs={{0,1},{1,2},{2,3},{3,0},{4,5},{5,6},{6,7},{7,4},{8,9},{9,10},{10,1... | collective-permute-start | bytes 1105928 | tf_op jit(solution)/shard_map/ppermute | solution.py:27
  56.5 19.1 %collective-permute-start.8 = (bf16[240,768]{1,0:T(8,128)(2,1)S(1)}, bf16[240,768]{1,0:T(8,128)(2,1)S(1)}, u32[]{:S(2)}, u32[]{:S(2)}) collective-permute-start(bf16[240,768]{1,0:T(8,128)(2,1)S(1)} %convolution_convert_fusion.1.refs_1_), channel_id=1, source_target_pairs={{0,1},{1,2},{2,3},{3,0},{4,5},{5,6},{6,7},{7,4},{8,9},{9,10},{10,1... | collective-permute-start | bytes 1105928 | tf_op jit(solution)/shard_map/ppermute | solution.py:27
  56.6 20.7 %collective-permute-start.7 = (bf16[240,768]{1,0:T(8,128)(2,1)S(1)}, bf16[240,768]{1,0:T(8,128)(2,1)S(1)}, u32[]{:S(2)}, u32[]{:S(2)}) collective-permute-start(bf16[240,768]{1,0:T(8,128)(2,1)S(1)} %convolution_convert_fusion.2.refs_0_), channel_id=1, source_target_pairs={{0,3},{1,0},{2,1},{3,2},{4,7},{5,4},{6,5},{7,6},{8,11},{9,8},{10,9... | collective-permute-start | bytes 1105928 | tf_op jit(solution)/shard_map/ppermute | solution.py:27
  63.5 13.8 %collective-permute-start.12 = (bf16[240,768]{1,0:T(8,128)(2,1)S(1)}, bf16[240,768]{1,0:T(8,128)(2,1)S(1)}, u32[]{:S(2)}, u32[]{:S(2)}) collective-permute-start(bf16[240,768]{1,0:T(8,128)(2,1)S(1)} %collective-permute-done.3.refs_1_), channel_id=1, source_target_pairs={{0,4},{4,0},{1,5},{5,1},{2,6},{6,2},{3,7},{7,3},{8,12},{12,8},{9,1... | collective-permute-start | bytes 1105928 | tf_op jit(solution)/shard_map/ppermute | solution.py:22
  65.0 14.3 %collective-permute-start.4 = (bf16[240,768]{1,0:T(8,128)(2,1)S(1)}, bf16[240,768]{1,0:T(8,128)(2,1)S(1)}, u32[]{:S(2)}, u32[]{:S(2)}) collective-permute-start(bf16[240,768]{1,0:T(8,128)(2,1)S(1)} %collective-permute-done.3.refs_1_), channel_id=1, source_target_pairs={{0,3},{1,0},{2,1},{3,2},{4,7},{5,4},{6,5},{7,6},{8,11},{9,8},{10,9... | collective-permute-start | bytes 1105928 | tf_op jit(solution)/shard_map/ppermute | solution.py:27
  68.4 15.2 %collective-permute-start.2 = (bf16[240,768]{1,0:T(8,128)(2,1)S(1)}, bf16[240,768]{1,0:T(8,128)(2,1)S(1)}, u32[]{:S(2)}, u32[]{:S(2)}) collective-permute-start(bf16[240,768]{1,0:T(8,128)(2,1)S(1)} %collective-permute-done.1.refs_0_), channel_id=1, source_target_pairs={{0,1},{1,2},{2,3},{3,0},{4,5},{5,6},{6,7},{7,4},{8,9},{9,10},{10,1... | collective-permute-start | bytes 1105928 | tf_op jit(solution)/shard_map/ppermute | solution.py:27
  75.6 9.8 %collective-permute-start.11 = (bf16[240,768]{1,0:T(8,128)(2,1)S(1)}, bf16[240,768]{1,0:T(8,128)(2,1)S(1)}, u32[]{:S(2)}, u32[]{:S(2)}) collective-permute-start(bf16[240,768]{1,0:T(8,128)(2,1)S(1)} %collective-permute-done.1.refs_0_), channel_id=1, source_target_pairs={{0,4},{4,0},{1,5},{5,1},{2,6},{6,2},{3,7},{7,3},{8,12},{12,8},{9,1... | collective-permute-start | bytes 1105928 | tf_op jit(solution)/shard_map/ppermute | solution.py:22
  77.2 9.2 %collective-permute-start.10 = (bf16[240,768]{1,0:T(8,128)(2,1)S(1)}, bf16[240,768]{1,0:T(8,128)(2,1)S(1)}, u32[]{:S(2)}, u32[]{:S(2)}) collective-permute-start(bf16[240,768]{1,0:T(8,128)(2,1)S(1)} %collective-permute-done.8.refs_1_), channel_id=1, source_target_pairs={{0,4},{4,0},{1,5},{5,1},{2,6},{6,2},{3,7},{7,3},{8,12},{12,8},{9,1... | collective-permute-start | bytes 1105928 | tf_op jit(solution)/shard_map/ppermute | solution.py:22
  77.2 9.2 %collective-permute-start.9 = (bf16[240,768]{1,0:T(8,128)(2,1)S(1)}, bf16[240,768]{1,0:T(8,128)(2,1)S(1)}, u32[]{:S(2)}, u32[]{:S(2)}) collective-permute-start(bf16[240,768]{1,0:T(8,128)(2,1)S(1)} %collective-permute-done.7.refs_0_), channel_id=1, source_target_pairs={{0,4},{4,0},{1,5},{5,1},{2,6},{6,2},{3,7},{7,3},{8,12},{12,8},{9,1... | collective-permute-start | bytes 1105928 | tf_op jit(solution)/shard_map/ppermute | solution.py:22
  79.2 8.2 %collective-permute-start.6 = (bf16[240,768]{1,0:T(8,128)(2,1)S(1)}, bf16[240,768]{1,0:T(8,128)(2,1)S(1)}, u32[]{:S(2)}, u32[]{:S(2)}) collective-permute-start(bf16[240,768]{1,0:T(8,128)(2,1)S(1)} %collective-permute-done.4.refs_1_), channel_id=1, source_target_pairs={{0,4},{4,0},{1,5},{5,1},{2,6},{6,2},{3,7},{7,3},{8,12},{12,8},{9,1... | collective-permute-start | bytes 1105928 | tf_op jit(solution)/shard_map/ppermute | solution.py:22
  91.6 13.9 %collective-permute-start.15 = (bf16[480,768]{1,0:T(8,128)(2,1)S(1)}, bf16[480,768]{1,0:T(8,128)(2,1)S(1)}, u32[]{:S(2)}, u32[]{:S(2)}) collective-permute-start(bf16[480,768]{1,0:T(8,128)(2,1)S(1)} %get-tuple-element.36), channel_id=1, source_target_pairs={{0,4},{4,0},{1,5},{5,1},{2,6},{6,2},{3,7},{7,3},{8,12},{12,8},{9,1... | collective-permute-start | bytes 2211848 | tf_op jit(solution)/shard_map/ppermute | solution.py:22
  93.3 10.1 %collective-permute-start.23 = (bf16[240,768]{1,0:T(8,128)(2,1)S(1)}, bf16[240,768]{1,0:T(8,128)(2,1)S(1)}, u32[]{:S(2)}, u32[]{:S(2)}) collective-permute-start(bf16[240,768]{1,0:T(8,128)(2,1)S(1)} %get-tuple-element.48), channel_id=1, source_target_pairs={{0,3},{1,0},{2,1},{3,2},{4,7},{5,4},{6,5},{7,6},{8,11},{9,8},{10,9... | collective-permute-start | bytes 1105928 | tf_op jit(solution)/shard_map/ppermute | solution.py:27
  93.4 11.7 %collective-permute-start.18 = (bf16[240,768]{1,0:T(8,128)(2,1)S(1)}, bf16[240,768]{1,0:T(8,128)(2,1)S(1)}, u32[]{:S(2)}, u32[]{:S(2)}) collective-permute-start(bf16[240,768]{1,0:T(8,128)(2,1)S(1)} %get-tuple-element.42), channel_id=1, source_target_pairs={{0,1},{1,2},{2,3},{3,0},{4,5},{5,6},{6,7},{7,4},{8,9},{9,10},{10,1... | collective-permute-start | bytes 1105928 | tf_op jit(solution)/shard_map/ppermute | solution.py:27
  95.5 17.2 %collective-permute-start.22 = (bf16[240,768]{1,0:T(8,128)(2,1)S(1)}, bf16[240,768]{1,0:T(8,128)(2,1)S(1)}, u32[]{:S(2)}, u32[]{:S(2)}) collective-permute-start(bf16[240,768]{1,0:T(8,128)(2,1)S(1)} %get-tuple-element.46), channel_id=1, source_target_pairs={{0,1},{1,2},{2,3},{3,0},{4,5},{5,6},{6,7},{7,4},{8,9},{9,10},{10,1... | collective-permute-start | bytes 1105928 | tf_op jit(solution)/shard_map/ppermute | solution.py:27
  95.5 17.1 %collective-permute-start.21 = (bf16[240,768]{1,0:T(8,128)(2,1)S(1)}, bf16[240,768]{1,0:T(8,128)(2,1)S(1)}, u32[]{:S(2)}, u32[]{:S(2)}) collective-permute-start(bf16[240,768]{1,0:T(8,128)(2,1)S(1)} %get-tuple-element.45), channel_id=1, source_target_pairs={{0,3},{1,0},{2,1},{3,2},{4,7},{5,4},{6,5},{7,6},{8,11},{9,8},{10,9... | collective-permute-start | bytes 1105928 | tf_op jit(solution)/shard_map/ppermute | solution.py:27
  103.5 15.7 %collective-permute-start.24 = (bf16[240,768]{1,0:T(8,128)(2,1)S(1)}, bf16[240,768]{1,0:T(8,128)(2,1)S(1)}, u32[]{:S(2)}, u32[]{:S(2)}) collective-permute-start(bf16[240,768]{1,0:T(8,128)(2,1)S(1)} %add_convert_fusion.1), channel_id=1, source_target_pairs={{0,3},{1,0},{2,1},{3,2},{4,7},{5,4},{6,5},{7,6},{8,11},{9,8},{10,9... | collective-permute-start | bytes 1105928 | tf_op jit(solution)/shard_map/ppermute | solution.py:27
  105.2 15.3 %collective-permute-start.19 = (bf16[240,768]{1,0:T(8,128)(2,1)S(1)}, bf16[240,768]{1,0:T(8,128)(2,1)S(1)}, u32[]{:S(2)}, u32[]{:S(2)}) collective-permute-start(bf16[240,768]{1,0:T(8,128)(2,1)S(1)} %add_convert_fusion.5), channel_id=1, source_target_pairs={{0,1},{1,2},{2,3},{3,0},{4,5},{5,6},{6,7},{7,4},{8,9},{9,10},{10,1... | collective-permute-start | bytes 1105928 | tf_op jit(solution)/shard_map/ppermute | solution.py:27
  122.8 31.6 %all-to-all-start.1 = ((bf16[32,24,768]{2,1,0:T(8,128)(2,1)}), bf16[32,24,768]{2,1,0:T(8,128)(2,1)S(1)}, u32[]{:S(2)}, u32[]{:S(2)}) async-start(bf16[32,24,768]{2,1,0:T(8,128)(2,1)} %bitcast.7), calls=%async_computation.1 | async-start | bytes 2359296 | tf_op jit(solution)/shard_map/all_to_all | solution.py:296
  127.6 27.0 %collective-permute-start.25 = (f32[24,192]{1,0:T(8,128)S(1)}, f32[24,192]{1,0:T(8,128)S(1)}, u32[]{:S(2)}, u32[]{:S(2)}) collective-permute-start(f32[24,192]{1,0:T(8,128)S(1)} %select_reduce_fusion), channel_id=1, source_target_pairs={{0,4},{4,0},{1,5},{5,1},{2,6},{6,2},{3,7},{7,3},{8,12},{12,8},{9,1... | collective-permute-start | bytes 55304 | tf_op jit(solution)/shard_map/ppermute | solution.py:22
  155.0 5.7 %collective-permute-start.26 = (bf16[24,768]{1,0:T(8,128)(2,1)S(1)}, bf16[24,768]{1,0:T(8,128)(2,1)S(1)}, u32[]{:S(2)}, u32[]{:S(2)}) collective-permute-start(bf16[24,768]{1,0:T(8,128)(2,1)S(1)} %convolution_convert_fusion.3), channel_id=1, source_target_pairs={{0,4},{4,0},{1,5},{5,1},{2,6},{6,2},{3,7},{7,3},{8,12},{12,8},{9,1... | collective-permute-start | bytes 110600 | tf_op jit(solution)/shard_map/ppermute | solution.py:22
  (10 other events, 95.2 us)

commit v2 on v1

--- a/solution.py
+++ b/solution.py
@@ -119,9 +119,9 @@
         gate_in, up_in = refs[:2]
         refs = refs[2:]
     if sends:
-        down_w = refs[0]
-        outs = refs[1 : 1 + len(sends)]
-        gate_acc, up_acc = refs[1 + len(sends) :]
+        down_w, hidden_ref = refs[:2]
+        outs = refs[2 : 2 + len(sends)]
+        gate_acc, up_acc = refs[2 + len(sends) :]
     else:
         gate_acc, up_acc = refs
     block = xs[0].shape[1]
@@ -145,9 +145,32 @@
         return
     gate = gate_acc[...]
     hidden = (gate / (1.0 + jnp.exp(-gate)) * up_acc[...]).astype(BF)
+    hidden_ref[...] = hidden
+    project(hidden, down_w, sends, outs)
+
+
+def project(hidden, down_w, sends, outs):
+    block = outs[0].shape[1]
     for j, at in enumerate(sends):
         cols = pl.ds(pl.multiple_of(column(at) * block, 128), block)
         outs[j][...] = jnp.dot(hidden, down_w[:, cols], preferred_element_type=F32).astype(BF)
+
+
+def down(hidden, down_rows, sends, block):
+    def body(hidden_ref, down_w, *outs):
+        project(hidden_ref[...], down_w, sends, outs)
+
+    rows, units = hidden.shape
+    n = len(sends)
+    return pl.pallas_call(
+        body,
+        out_shape=[pltpu.VMEM((rows, block), BF)] * n,
+        in_specs=[VMEM] * 2,
+        out_specs=[VMEM] * n,
+        compiler_params=pltpu.CompilerParams(vmem_limit_bytes=16 * 2**20),
+        cost_estimate=cost(2 * n * rows * units * block, (n, units, block), (n, rows, block)),
+        name="down",
+    )(near(hidden), near(down_rows))
 
 
 def gate_up(xs, pieces, ats, gate_rows, up_rows, carried, rows, down_rows=None, sends=()):
@@ -155,7 +178,8 @@
     units = gate_rows.shape[1]
     first = carried is None
     if sends:
-        out = [pltpu.VMEM((rows, block), BF)] * len(sends)
+        out = [pltpu.VMEM((rows, units), BF)]
+        out += [pltpu.VMEM((rows, block), BF)] * len(sends)
     else:
         out = [pltpu.VMEM((rows, units), F32)] * 2
     n = len(ats)
@@ -256,13 +280,16 @@
         )
     far = [far_top, far_bottom]
     order = (2, 1, -1, 0)
-    parts = gate_up(
+    hidden, *far_parts = gate_up(
         far + [swap_cores(v) for v in far],
         [(0, 0, mid), (0, mid, capacity), (1, 0, mid), (1, mid, capacity)],
         ((2, 0), (2, 1)),
         gate_rows, up_rows, acts, capacity,
-        down_rows, tuple((off, 1) for off in order) + tuple((off, 0) for off in order),
-    )
+        down_rows, ((2, 1), (2, 0)),
+    )
+    far_peer = swap_cores(far_parts[0])
+    rest = down(hidden, down_rows, tuple((off, peer) for peer in (1, 0) for off in order[1:]), half)
+    parts = [far_parts[0], *rest[:3], far_parts[1], *rest[3:]]
 
     def add(*values):
         return sum(v.astype(F32) for v in values).astype(BF)
@@ -272,7 +299,7 @@
             (add(parts[4 + k][:mid], peer[:mid]), add(parts[4 + k][mid:], peer[mid:]))
         )
 
-    peers = [swap_cores(v) for v in parts[:4]]
+    peers = [far_peer] + [swap_cores(v) for v in rest[:3]]
     far_top, far_bottom = chip_sums(0, peers[0])
     top_in = shift_y(far_top, 1)
     bottom_in = shift_y(far_bottom, -1)

time: 162 us -> 161 us (level)
  transfers between devices with their start and end apart: 28 -> 28, of which waited for: 13 -> 12; matrix products, arithmetic and copies ran while one was open for 1% -> 1% of each run, Pallas kernels for 2% -> 3%
where the time goes in v2:
time: 161 us; the launch traced here: 160 us
  waiting for transfers between devices  64.3 us (40%)
  blocking collectives  40.9 us (25%)
  starting transfers between devices  37.6 us (23%)
  Pallas kernels  6.41 us (4%)
  local copies, waits for them, and re-layouts  3.65 us (2%)
  other arithmetic  3.64 us (2%)
  matrix products  3.58 us (2%)
    all_to_all x1, blocking collectives, layer(): lax.all_to_all(spread.reshape(chips, *blocks.shape[1:]), ('x', 'z'), 0, 0...  40.9 us
    ppermute x12, waiting for transfers between devices, shift(): lax.ppermute(value, axis, [(i, (i + by) % size) for i in range(size)])  36.3 us
    all_to_all x1, waiting for transfers between devices, layer(): lax.all_to_all(back.reshape(chips, rows, half), ('x', 'z'), 0, 0, tiled=T...  25.8 us
    ppermute x15, starting transfers between devices, swap_cores(): return lax.ppermute(value, 'c', SWAP)  18.5 us
    ppermute x12, starting transfers between devices, shift(): lax.ppermute(value, axis, [(i, (i + by) % size) for i in range(size)])  15 us
    pallas_call x4, Pallas kernels, gate_up(): pl.pallas_call(body, out_shape=out, in_specs=[VMEM] * len(inputs), out_sp...  4.17 us
    all_to_all x1, starting transfers between devices, layer(): lax.all_to_all(back.reshape(chips, rows, half), ('x', 'z'), 0, 0, tiled=T...  4.07 us
  transfers between devices with their start and end apart: 28, of which 12 were waited for; matrix products, arithmetic and copies ran while one was open for 1% of the time, Pallas kernels for 3%

profile of v2, /device:TPU:1, one launch (start us, length us, event | category | flops | bytes accessed | tf_op | source)
XLA Modules:
  0.0 160.5 jit_solution(14328269767626897165)
XLA Ops:
  2.5 3.3 %collective-permute-start = (bf16[8,144,128]{2,1,0:T(8,128)(2,1)S(1)}, bf16[8,144,128]{2,1,0:T(8,128)(2,1)S(1)}, u32[]{:S(2)}, u32[]{:S(2)}) collective-permute-start(bf16[8,144,128]{2,1,0:T(8,128)(2,1)S(1)} %get-tuple-element.29), channel_id=1, source_target_pairs={{0,4},{4,0},{1,5},{5,1},{2,6},{6,2},{3,7},{7,3},{8,12},{12,8},{9,1... | collective-permute-start | bytes 884744 | tf_op jit(solution)/shard_map/ppermute | solution.py:22
  7.3 40.9 %all_to_all.10 = bf16[32,144,128]{2,1,0:T(8,128)(2,1)S(1)} all-to-all(bf16[32,144,128]{2,1,0:T(8,128)(2,1)S(1)} %bitcast.37), channel_id=1, replica_groups=mesh['x'=4,'z'=8,'c'=2,'y'=4] {'x','z'}, dimensions={0} | all-to-all | bytes 2359296 | tf_op jit(solution)/shard_map/all_to_all | solution.py:235
  50.7 2.2 %collective-permute-start.14 = (bf16[240,768]{1,0:T(8,128)(2,1)S(1)}, bf16[240,768]{1,0:T(8,128)(2,1)S(1)}, u32[]{:S(2)}, u32[]{:S(2)}) collective-permute-start(bf16[240,768]{1,0:T(8,128)(2,1)S(1)} %convolution_convert_fusion.1.refs_1_), channel_id=1, source_target_pairs={{0,4},{4,0},{1,5},{5,1},{2,6},{6,2},{3,7},{7,3},{8,12},{12,8},{9,1... | collective-permute-start | bytes 1105928 | tf_op jit(solution)/shard_map/ppermute | solution.py:22
  52.9 2.7 %collective-permute-start.3 = (bf16[240,768]{1,0:T(8,128)(2,1)S(1)}, bf16[240,768]{1,0:T(8,128)(2,1)S(1)}, u32[]{:S(2)}, u32[]{:S(2)}) collective-permute-start(bf16[240,768]{1,0:T(8,128)(2,1)S(1)} %convolution_convert_fusion.1.refs_1_), channel_id=1, source_target_pairs={{0,3},{1,0},{2,1},{3,2},{4,7},{5,4},{6,5},{7,6},{8,11},{9,8},{10,9... | collective-permute-start | bytes 1105928 | tf_op jit(solution)/shard_map/ppermute | solution.py:27
  56.6 2.7 %collective-permute-start.7 = (bf16[240,768]{1,0:T(8,128)(2,1)S(1)}, bf16[240,768]{1,0:T(8,128)(2,1)S(1)}, u32[]{:S(2)}, u32[]{:S(2)}) collective-permute-start(bf16[240,768]{1,0:T(8,128)(2,1)S(1)} %convolution_convert_fusion.2.refs_0_), channel_id=1, source_target_pairs={{0,3},{1,0},{2,1},{3,2},{4,7},{5,4},{6,5},{7,6},{8,11},{9,8},{10,9... | collective-permute-start | bytes 1105928 | tf_op jit(solution)/shard_map/ppermute | solution.py:27
  59.2 4.2 %collective-permute-done.3.refs_1_ = bf16[240,768]{1,0:T(8,128)(2,1)S(1)} collective-permute-done((bf16[240,768]{1,0:T(8,128)(2,1)S(1)}, bf16[240,768]{1,0:T(8,128)(2,1)S(1)}, u32[]{:S(2)}, u32[]{:S(2)}) %collective-permute-start.3) | collective-permute-done | bytes 368672 | tf_op jit(solution)/shard_map/ppermute | solution.py:27
  63.5 1.5 collective-permute-start.12
  65.0 3.4 %collective-permute-start.4 = (bf16[240,768]{1,0:T(8,128)(2,1)S(1)}, bf16[240,768]{1,0:T(8,128)(2,1)S(1)}, u32[]{:S(2)}, u32[]{:S(2)}) collective-permute-start(bf16[240,768]{1,0:T(8,128)(2,1)S(1)} %collective-permute-done.3.refs_1_), channel_id=1, source_target_pairs={{0,3},{1,0},{2,1},{3,2},{4,7},{5,4},{6,5},{7,6},{8,11},{9,8},{10,9... | collective-permute-start | bytes 1105928 | tf_op jit(solution)/shard_map/ppermute | solution.py:27
  68.4 7.3 %collective-permute-done.8.refs_1_ = bf16[240,768]{1,0:T(8,128)(2,1)S(1)} collective-permute-done((bf16[240,768]{1,0:T(8,128)(2,1)S(1)}, bf16[240,768]{1,0:T(8,128)(2,1)S(1)}, u32[]{:S(2)}, u32[]{:S(2)}) %collective-permute-start.8) | collective-permute-done | bytes 368672 | tf_op jit(solution)/shard_map/ppermute | solution.py:27
  75.6 1.6 collective-permute-start.11
  77.8 1.5 collective-permute-done.4.refs_1_
  80.2 3.3 %collective-permute-done.2.refs_0_ = bf16[240,768]{1,0:T(8,128)(2,1)S(1)} collective-permute-done((bf16[240,768]{1,0:T(8,128)(2,1)S(1)}, bf16[240,768]{1,0:T(8,128)(2,1)S(1)}, u32[]{:S(2)}, u32[]{:S(2)}) %collective-permute-start.2) | collective-permute-done | bytes 368672 | tf_op jit(solution)/shard_map/ppermute | solution.py:27
  88.4 1.4 gate_up_down.1
  89.8 1.3 down.1
  92.5 1.5 collective-permute-start.18
  94.9 2.7 %collective-permute-start.21 = (bf16[240,768]{1,0:T(8,128)(2,1)S(1)}, bf16[240,768]{1,0:T(8,128)(2,1)S(1)}, u32[]{:S(2)}, u32[]{:S(2)}) collective-permute-start(bf16[240,768]{1,0:T(8,128)(2,1)S(1)} %get-tuple-element.47), channel_id=1, source_target_pairs={{0,3},{1,0},{2,1},{3,2},{4,7},{5,4},{6,5},{7,6},{8,11},{9,8},{10,9... | collective-permute-start | bytes 1105928 | tf_op jit(solution)/shard_map/ppermute | solution.py:27
  97.6 5.0 %collective-permute-done.23 = bf16[240,768]{1,0:T(8,128)(2,1)S(1)} collective-permute-done((bf16[240,768]{1,0:T(8,128)(2,1)S(1)}, bf16[240,768]{1,0:T(8,128)(2,1)S(1)}, u32[]{:S(2)}, u32[]{:S(2)}) %collective-permute-start.23) | collective-permute-done | bytes 368672 | tf_op jit(solution)/shard_map/ppermute | solution.py:27
  102.6 1.6 collective-permute-start.24
  104.6 7.1 %collective-permute-done.22 = bf16[240,768]{1,0:T(8,128)(2,1)S(1)} collective-permute-done((bf16[240,768]{1,0:T(8,128)(2,1)S(1)}, bf16[240,768]{1,0:T(8,128)(2,1)S(1)}, u32[]{:S(2)}, u32[]{:S(2)}) %collective-permute-start.22) | collective-permute-done | bytes 368672 | tf_op jit(solution)/shard_map/ppermute | solution.py:27
  111.7 6.6 %collective-permute-done.24 = bf16[240,768]{1,0:T(8,128)(2,1)S(1)} collective-permute-done((bf16[240,768]{1,0:T(8,128)(2,1)S(1)}, bf16[240,768]{1,0:T(8,128)(2,1)S(1)}, u32[]{:S(2)}, u32[]{:S(2)}) %collective-permute-start.24) | collective-permute-done | bytes 368672 | tf_op jit(solution)/shard_map/ppermute | solution.py:27
  120.0 1.9 %convolution_convert_fusion = bf16[768,768]{1,0:T(8,128)(2,1)} fusion(bf16[240,768]{1,0:T(8,128)(2,1)S(1)} %get-tuple-element.52, bf16[240,768]{1,0:T(8,128)(2,1)S(1)} %get-tuple-element.51, s32[768]{0:T(1024)S(1)} %select_n.30), kind=kOutput, calls=%fused_computation.1 | convolution fusion | flops 568664064 | bytes 1920000 | tf_op jit(solution)/shard_map/dot_general | solution.py:320
  121.9 4.1 %all-to-all-start.1 = ((bf16[32,24,768]{2,1,0:T(8,128)(2,1)}), bf16[32,24,768]{2,1,0:T(8,128)(2,1)S(1)}, u32[]{:S(2)}, u32[]{:S(2)}) async-start(bf16[32,24,768]{2,1,0:T(8,128)(2,1)} %bitcast.7), calls=%async_computation.1 | async-start | bytes 2359296 | tf_op jit(solution)/shard_map/all_to_all | solution.py:323
  127.8 25.8 %all-to-all-done.1 = bf16[32,24,768]{2,1,0:T(8,128)(2,1)S(1)} async-done(((bf16[32,24,768]{2,1,0:T(8,128)(2,1)}), bf16[32,24,768]{2,1,0:T(8,128)(2,1)S(1)}, u32[]{:S(2)}, u32[]{:S(2)}) %all-to-all-start.1) | async-done | bytes 1179680 | tf_op jit(solution)/shard_map/all_to_all | solution.py:323
  154.1 4.8 %collective-permute-start.26 = (bf16[24,768]{1,0:T(8,128)(2,1)S(1)}, bf16[24,768]{1,0:T(8,128)(2,1)S(1)}, u32[]{:S(2)}, u32[]{:S(2)}) collective-permute-start(bf16[24,768]{1,0:T(8,128)(2,1)S(1)} %convolution_convert_fusion.3), channel_id=1, source_target_pairs={{0,4},{4,0},{1,5},{5,1},{2,6},{6,2},{3,7},{7,3},{8,12},{12,8},{9,1... | collective-permute-start | bytes 110600 | tf_op jit(solution)/shard_map/ppermute | solution.py:22
  (87 shorter events, 21.9 us)
Async XLA Ops:
  2.5 4.5 %collective-permute-start = (bf16[8,144,128]{2,1,0:T(8,128)(2,1)S(1)}, bf16[8,144,128]{2,1,0:T(8,128)(2,1)S(1)}, u32[]{:S(2)}, u32[]{:S(2)}) collective-permute-start(bf16[8,144,128]{2,1,0:T(8,128)(2,1)S(1)} %get-tuple-element.29), channel_id=1, source_target_pairs={{0,4},{4,0},{1,5},{5,1},{2,6},{6,2},{3,7},{7,3},{8,12},{12,8},{9,1... | collective-permute-start | bytes 884744 | tf_op jit(solution)/shard_map/ppermute | solution.py:22
  50.7 5.9 %collective-permute-start.14 = (bf16[240,768]{1,0:T(8,128)(2,1)S(1)}, bf16[240,768]{1,0:T(8,128)(2,1)S(1)}, u32[]{:S(2)}, u32[]{:S(2)}) collective-permute-start(bf16[240,768]{1,0:T(8,128)(2,1)S(1)} %convolution_convert_fusion.1.refs_1_), channel_id=1, source_target_pairs={{0,4},{4,0},{1,5},{5,1},{2,6},{6,2},{3,7},{7,3},{8,12},{12,8},{9,1... | collective-permute-start | bytes 1105928 | tf_op jit(solution)/shard_map/ppermute | solution.py:22
  52.9 10.6 %collective-permute-start.3 = (bf16[240,768]{1,0:T(8,128)(2,1)S(1)}, bf16[240,768]{1,0:T(8,128)(2,1)S(1)}, u32[]{:S(2)}, u32[]{:S(2)}) collective-permute-start(bf16[240,768]{1,0:T(8,128)(2,1)S(1)} %convolution_convert_fusion.1.refs_1_), channel_id=1, source_target_pairs={{0,3},{1,0},{2,1},{3,2},{4,7},{5,4},{6,5},{7,6},{8,11},{9,8},{10,9... | collective-permute-start | bytes 1105928 | tf_op jit(solution)/shard_map/ppermute | solution.py:27
  56.1 8.9 %collective-permute-start.13 = (bf16[240,768]{1,0:T(8,128)(2,1)S(1)}, bf16[240,768]{1,0:T(8,128)(2,1)S(1)}, u32[]{:S(2)}, u32[]{:S(2)}) collective-permute-start(bf16[240,768]{1,0:T(8,128)(2,1)S(1)} %convolution_convert_fusion.2.refs_0_), channel_id=1, source_target_pairs={{0,4},{4,0},{1,5},{5,1},{2,6},{6,2},{3,7},{7,3},{8,12},{12,8},{9,1... | collective-permute-start | bytes 1105928 | tf_op jit(solution)/shard_map/ppermute | solution.py:22
  56.5 11.8 %collective-permute-start.1 = (bf16[240,768]{1,0:T(8,128)(2,1)S(1)}, bf16[240,768]{1,0:T(8,128)(2,1)S(1)}, u32[]{:S(2)}, u32[]{:S(2)}) collective-permute-start(bf16[240,768]{1,0:T(8,128)(2,1)S(1)} %convolution_convert_fusion.2.refs_0_), channel_id=1, source_target_pairs={{0,1},{1,2},{2,3},{3,0},{4,5},{5,6},{6,7},{7,4},{8,9},{9,10},{10,1... | collective-permute-start | bytes 1105928 | tf_op jit(solution)/shard_map/ppermute | solution.py:27
  56.5 19.1 %collective-permute-start.8 = (bf16[240,768]{1,0:T(8,128)(2,1)S(1)}, bf16[240,768]{1,0:T(8,128)(2,1)S(1)}, u32[]{:S(2)}, u32[]{:S(2)}) collective-permute-start(bf16[240,768]{1,0:T(8,128)(2,1)S(1)} %convolution_convert_fusion.1.refs_1_), channel_id=1, source_target_pairs={{0,1},{1,2},{2,3},{3,0},{4,5},{5,6},{6,7},{7,4},{8,9},{9,10},{10,1... | collective-permute-start | bytes 1105928 | tf_op jit(solution)/shard_map/ppermute | solution.py:27
  56.6 20.7 %collective-permute-start.7 = (bf16[240,768]{1,0:T(8,128)(2,1)S(1)}, bf16[240,768]{1,0:T(8,128)(2,1)S(1)}, u32[]{:S(2)}, u32[]{:S(2)}) collective-permute-start(bf16[240,768]{1,0:T(8,128)(2,1)S(1)} %convolution_convert_fusion.2.refs_0_), channel_id=1, source_target_pairs={{0,3},{1,0},{2,1},{3,2},{4,7},{5,4},{6,5},{7,6},{8,11},{9,8},{10,9... | collective-permute-start | bytes 1105928 | tf_op jit(solution)/shard_map/ppermute | solution.py:27
  63.5 13.8 %collective-permute-start.12 = (bf16[240,768]{1,0:T(8,128)(2,1)S(1)}, bf16[240,768]{1,0:T(8,128)(2,1)S(1)}, u32[]{:S(2)}, u32[]{:S(2)}) collective-permute-start(bf16[240,768]{1,0:T(8,128)(2,1)S(1)} %collective-permute-done.3.refs_1_), channel_id=1, source_target_pairs={{0,4},{4,0},{1,5},{5,1},{2,6},{6,2},{3,7},{7,3},{8,12},{12,8},{9,1... | collective-permute-start | bytes 1105928 | tf_op jit(solution)/shard_map/ppermute | solution.py:22
  65.0 14.3 %collective-permute-start.4 = (bf16[240,768]{1,0:T(8,128)(2,1)S(1)}, bf16[240,768]{1,0:T(8,128)(2,1)S(1)}, u32[]{:S(2)}, u32[]{:S(2)}) collective-permute-start(bf16[240,768]{1,0:T(8,128)(2,1)S(1)} %collective-permute-done.3.refs_1_), channel_id=1, source_target_pairs={{0,3},{1,0},{2,1},{3,2},{4,7},{5,4},{6,5},{7,6},{8,11},{9,8},{10,9... | collective-permute-start | bytes 1105928 | tf_op jit(solution)/shard_map/ppermute | solution.py:27
  68.4 15.2 %collective-permute-start.2 = (bf16[240,768]{1,0:T(8,128)(2,1)S(1)}, bf16[240,768]{1,0:T(8,128)(2,1)S(1)}, u32[]{:S(2)}, u32[]{:S(2)}) collective-permute-start(bf16[240,768]{1,0:T(8,128)(2,1)S(1)} %collective-permute-done.1.refs_0_), channel_id=1, source_target_pairs={{0,1},{1,2},{2,3},{3,0},{4,5},{5,6},{6,7},{7,4},{8,9},{9,10},{10,1... | collective-permute-start | bytes 1105928 | tf_op jit(solution)/shard_map/ppermute | solution.py:27
  75.6 9.8 %collective-permute-start.11 = (bf16[240,768]{1,0:T(8,128)(2,1)S(1)}, bf16[240,768]{1,0:T(8,128)(2,1)S(1)}, u32[]{:S(2)}, u32[]{:S(2)}) collective-permute-start(bf16[240,768]{1,0:T(8,128)(2,1)S(1)} %collective-permute-done.1.refs_0_), channel_id=1, source_target_pairs={{0,4},{4,0},{1,5},{5,1},{2,6},{6,2},{3,7},{7,3},{8,12},{12,8},{9,1... | collective-permute-start | bytes 1105928 | tf_op jit(solution)/shard_map/ppermute | solution.py:22
  77.2 9.2 %collective-permute-start.10 = (bf16[240,768]{1,0:T(8,128)(2,1)S(1)}, bf16[240,768]{1,0:T(8,128)(2,1)S(1)}, u32[]{:S(2)}, u32[]{:S(2)}) collective-permute-start(bf16[240,768]{1,0:T(8,128)(2,1)S(1)} %collective-permute-done.8.refs_1_), channel_id=1, source_target_pairs={{0,4},{4,0},{1,5},{5,1},{2,6},{6,2},{3,7},{7,3},{8,12},{12,8},{9,1... | collective-permute-start | bytes 1105928 | tf_op jit(solution)/shard_map/ppermute | solution.py:22
  77.2 9.2 %collective-permute-start.9 = (bf16[240,768]{1,0:T(8,128)(2,1)S(1)}, bf16[240,768]{1,0:T(8,128)(2,1)S(1)}, u32[]{:S(2)}, u32[]{:S(2)}) collective-permute-start(bf16[240,768]{1,0:T(8,128)(2,1)S(1)} %collective-permute-done.7.refs_0_), channel_id=1, source_target_pairs={{0,4},{4,0},{1,5},{5,1},{2,6},{6,2},{3,7},{7,3},{8,12},{12,8},{9,1... | collective-permute-start | bytes 1105928 | tf_op jit(solution)/shard_map/ppermute | solution.py:22
  79.2 8.2 %collective-permute-start.6 = (bf16[240,768]{1,0:T(8,128)(2,1)S(1)}, bf16[240,768]{1,0:T(8,128)(2,1)S(1)}, u32[]{:S(2)}, u32[]{:S(2)}) collective-permute-start(bf16[240,768]{1,0:T(8,128)(2,1)S(1)} %collective-permute-done.4.refs_1_), channel_id=1, source_target_pairs={{0,4},{4,0},{1,5},{5,1},{2,6},{6,2},{3,7},{7,3},{8,12},{12,8},{9,1... | collective-permute-start | bytes 1105928 | tf_op jit(solution)/shard_map/ppermute | solution.py:22
  91.8 12.8 %collective-permute-start.15 = (bf16[480,768]{1,0:T(8,128)(2,1)S(1)}, bf16[480,768]{1,0:T(8,128)(2,1)S(1)}, u32[]{:S(2)}, u32[]{:S(2)}) collective-permute-start(bf16[480,768]{1,0:T(8,128)(2,1)S(1)} %get-tuple-element.38), channel_id=1, source_target_pairs={{0,4},{4,0},{1,5},{5,1},{2,6},{6,2},{3,7},{7,3},{8,12},{12,8},{9,1... | collective-permute-start | bytes 2211848 | tf_op jit(solution)/shard_map/ppermute | solution.py:22
  92.4 10.1 %collective-permute-start.23 = (bf16[240,768]{1,0:T(8,128)(2,1)S(1)}, bf16[240,768]{1,0:T(8,128)(2,1)S(1)}, u32[]{:S(2)}, u32[]{:S(2)}) collective-permute-start(bf16[240,768]{1,0:T(8,128)(2,1)S(1)} %get-tuple-element.50), channel_id=1, source_target_pairs={{0,3},{1,0},{2,1},{3,2},{4,7},{5,4},{6,5},{7,6},{8,11},{9,8},{10,9... | collective-permute-start | bytes 1105928 | tf_op jit(solution)/shard_map/ppermute | solution.py:27
  92.5 11.7 %collective-permute-start.18 = (bf16[240,768]{1,0:T(8,128)(2,1)S(1)}, bf16[240,768]{1,0:T(8,128)(2,1)S(1)}, u32[]{:S(2)}, u32[]{:S(2)}) collective-permute-start(bf16[240,768]{1,0:T(8,128)(2,1)S(1)} %get-tuple-element.44), channel_id=1, source_target_pairs={{0,1},{1,2},{2,3},{3,0},{4,5},{5,6},{6,7},{7,4},{8,9},{9,10},{10,1... | collective-permute-start | bytes 1105928 | tf_op jit(solution)/shard_map/ppermute | solution.py:27
  94.8 16.9 %collective-permute-start.22 = (bf16[240,768]{1,0:T(8,128)(2,1)S(1)}, bf16[240,768]{1,0:T(8,128)(2,1)S(1)}, u32[]{:S(2)}, u32[]{:S(2)}) collective-permute-start(bf16[240,768]{1,0:T(8,128)(2,1)S(1)} %get-tuple-element.48), channel_id=1, source_target_pairs={{0,1},{1,2},{2,3},{3,0},{4,5},{5,6},{6,7},{7,4},{8,9},{9,10},{10,1... | collective-permute-start | bytes 1105928 | tf_op jit(solution)/shard_map/ppermute | solution.py:27
  94.9 16.9 %collective-permute-start.21 = (bf16[240,768]{1,0:T(8,128)(2,1)S(1)}, bf16[240,768]{1,0:T(8,128)(2,1)S(1)}, u32[]{:S(2)}, u32[]{:S(2)}) collective-permute-start(bf16[240,768]{1,0:T(8,128)(2,1)S(1)} %get-tuple-element.47), channel_id=1, source_target_pairs={{0,3},{1,0},{2,1},{3,2},{4,7},{5,4},{6,5},{7,6},{8,11},{9,8},{10,9... | collective-permute-start | bytes 1105928 | tf_op jit(solution)/shard_map/ppermute | solution.py:27
  102.6 15.7 %collective-permute-start.24 = (bf16[240,768]{1,0:T(8,128)(2,1)S(1)}, bf16[240,768]{1,0:T(8,128)(2,1)S(1)}, u32[]{:S(2)}, u32[]{:S(2)}) collective-permute-start(bf16[240,768]{1,0:T(8,128)(2,1)S(1)} %add_convert_fusion.1), channel_id=1, source_target_pairs={{0,3},{1,0},{2,1},{3,2},{4,7},{5,4},{6,5},{7,6},{8,11},{9,8},{10,9... | collective-permute-start | bytes 1105928 | tf_op jit(solution)/shard_map/ppermute | solution.py:27
  104.3 15.3 %collective-permute-start.19 = (bf16[240,768]{1,0:T(8,128)(2,1)S(1)}, bf16[240,768]{1,0:T(8,128)(2,1)S(1)}, u32[]{:S(2)}, u32[]{:S(2)}) collective-permute-start(bf16[240,768]{1,0:T(8,128)(2,1)S(1)} %add_convert_fusion.5), channel_id=1, source_target_pairs={{0,1},{1,2},{2,3},{3,0},{4,5},{5,6},{6,7},{7,4},{8,9},{9,10},{10,1... | collective-permute-start | bytes 1105928 | tf_op jit(solution)/shard_map/ppermute | solution.py:27
  121.9 31.6 %all-to-all-start.1 = ((bf16[32,24,768]{2,1,0:T(8,128)(2,1)}), bf16[32,24,768]{2,1,0:T(8,128)(2,1)S(1)}, u32[]{:S(2)}, u32[]{:S(2)}) async-start(bf16[32,24,768]{2,1,0:T(8,128)(2,1)} %bitcast.7), calls=%async_computation.1 | async-start | bytes 2359296 | tf_op jit(solution)/shard_map/all_to_all | solution.py:323
  126.7 27.0 %collective-permute-start.25 = (f32[24,192]{1,0:T(8,128)S(1)}, f32[24,192]{1,0:T(8,128)S(1)}, u32[]{:S(2)}, u32[]{:S(2)}) collective-permute-start(f32[24,192]{1,0:T(8,128)S(1)} %select_reduce_fusion), channel_id=1, source_target_pairs={{0,4},{4,0},{1,5},{5,1},{2,6},{6,2},{3,7},{7,3},{8,12},{12,8},{9,1... | collective-permute-start | bytes 55304 | tf_op jit(solution)/shard_map/ppermute | solution.py:22
  154.1 5.7 %collective-permute-start.26 = (bf16[24,768]{1,0:T(8,128)(2,1)S(1)}, bf16[24,768]{1,0:T(8,128)(2,1)S(1)}, u32[]{:S(2)}, u32[]{:S(2)}) collective-permute-start(bf16[24,768]{1,0:T(8,128)(2,1)S(1)} %convolution_convert_fusion.3), channel_id=1, source_target_pairs={{0,4},{4,0},{1,5},{5,1},{2,6},{6,2},{3,7},{7,3},{8,12},{12,8},{9,1... | collective-permute-start | bytes 110600 | tf_op jit(solution)/shard_map/ppermute | solution.py:22
  (10 other events, 93.4 us)
